TPU v7x, 256 devices: a whole 4x4x8 slice. The times are simulated.
256 devices in a mesh: gx: 8 (over z), gy: 4 (over x), gz: 8 (over y, core).
Axes of the slice: x: 4, y: 4, z: 8, core: 2. Of those that a mesh axis runs over, the one named last changes fastest.
Arguments:
- patch_logits: bfloat16 [8, 4, 8, 24, 20736], P('gx', 'gy', 'gz'), may hold values from -12 to 312
- patch_start: int32 [8, 4, 8, 3], replicated, may hold values from 0 to 880, as said below
- patch_owner: int32 [8, 4, 8], replicated, may hold values from 0 to 31, as said below
Outputs:
- probs: float32 [64, 128, 3, 1024], P('gx', 'gy', None, 'gz')
Inputs may be any that keep to these rules, and one draw needn't show every extreme that they name: `patch_start`: entry [i, j, k, d] is the first cell along dimension d of the patch at lattice position (i, j, k): i * 8 - 8 along x (32 and 128 in place of 8 along y and z), moved by at most 4 cells, then moved inward so that the patch lies inside the volume. `patch_owner`: for every k the entries [:, :, k] are the numbers 0 to 31, each once.
All inputs are finite; a program needn't handle non-finite values.
Results may differ from a plain program's by a relative error of at most 0.0003.
Values may be sent and summed in bfloat16 or wider, within the bound.
A program may use at most 128 MiB of HBM per device.

v0:
```python
import jax
import jax.numpy as jnp
from jax import lax
from jax.sharding import PartitionSpec as P

CLASSES = 3
BX = 8
BY = 32
BZ = 128
HALO = 8
PX = 24
PY = 48
PZ = 144


def extended(x, sides, width):
    for axis, dim in sides:
        size, length = (lax.axis_size(axis), x.shape[dim])
        up = [(i, (i + 1) % size) for i in range(size - 1)]
        down = [(j, i) for i, j in up]
        last = lax.slice_in_dim(x, length - width, length, axis=dim)
        first = lax.slice_in_dim(x, 0, width, axis=dim)
        before = lax.ppermute(last, axis, up)
        after = lax.ppermute(first, axis, down)
        x = jnp.concatenate([before, x, after], axis=dim)
    return x


def profile(offsets, length):
    inside = (offsets >= 0) & (offsets < length)
    centre = (length - 1) / 2.0
    spread = length / 4.0
    values = jnp.exp(-((offsets.astype(jnp.float32) - centre) ** 2) / (2.0 * spread * spread))
    return jnp.where(inside, values, 0.0)


def fold_rims(padded, block_len, margin):
    centre = padded[..., 2 * margin : 2 * margin + block_len]
    below_rim = padded[..., :margin]
    above_rim = padded[..., block_len + 3 * margin :]
    widths_low = [(0, 0)] * (padded.ndim - 1) + [(0, block_len - margin)]
    widths_high = [(0, 0)] * (padded.ndim - 1) + [(block_len - margin, 0)]
    return centre + jnp.pad(below_rim, widths_low) + jnp.pad(above_rim, widths_high)


def finish(canvas, weight_sum):
    padded = extended(canvas, (("gz", 3),), 2 * HALO)
    summed = fold_rims(padded, BZ, 2 * HALO)
    scores = summed / weight_sum[:, :, None, :]
    return jax.nn.softmax(scores, axis=2)


def local_weights(patch_start, anchor_x, anchor_y, anchor_z):
    patches = patch_start.shape[0] * patch_start.shape[1] * patch_start.shape[2]
    starts = patch_start.reshape(patches, 3)
    along_x = profile(anchor_x + jnp.arange(BX)[None, :] - starts[:, 0:1], PX)
    along_y = profile(anchor_y + jnp.arange(BY)[None, :] - starts[:, 1:2], PY)
    along_z = profile(anchor_z + jnp.arange(BZ)[None, :] - starts[:, 2:3], PZ)
    xy_plane = (along_x[:, :, None] * along_y[:, None, :]).reshape(patches, BX * BY)
    summed = jnp.einsum("pa,pz->az", xy_plane, along_z, precision=lax.Precision.HIGHEST)
    return summed.reshape(BX, BY, BZ)


def pad_patch(source, margin):
    return jnp.pad(source, ((BX, BX), (BY, BY), (0, 0), (margin, 2 * margin)))


def owner_block(padded, target, lanes_y, corner, shift_z, window):
    start_x = jnp.clip(target // lanes_y * BX - corner[0] + BX, 0, PX + BX)
    start_y = jnp.clip(target % lanes_y * BY - corner[1] + BY, 0, PY + BY)
    start_z = 2 * HALO - shift_z
    return lax.dynamic_slice(
        padded, (start_x, start_y, jnp.int32(0), start_z), (BX, BY, padded.shape[2], window)
    )


def per_device(patch_logits, patch_start, patch_owner):
    lanes_y = lax.axis_size("gy")
    place_x = lax.axis_index("gx")
    place_y = lax.axis_index("gy")
    place_z = lax.axis_index("gz")
    classes = CLASSES
    logits = patch_logits[0, 0, 0].reshape(PX, PY, classes, PZ)
    margin = 2 * HALO
    window = BZ + 2 * margin
    anchor_x = place_x * BX
    anchor_y = place_y * BY
    anchor_z = place_z * BZ
    window_z = anchor_z - margin
    patch_code = patch_owner[place_x, place_y, place_z]
    corner = patch_start[patch_code // lanes_y, patch_code % lanes_y, place_z]
    shift_z = corner[2] - window_z
    weight_sum = local_weights(patch_start, anchor_x, anchor_y, anchor_z)
    along_x = profile(jnp.arange(PX), PX)
    along_y = profile(jnp.arange(PY), PY)
    along_z = profile(jnp.arange(PZ), PZ)
    weight = along_x[:, None, None, None] * along_y[None, :, None, None]
    weight = weight * along_z[None, None, None, :]
    blended = logits * weight
    padded = pad_patch(blended, margin)
    targets = jnp.arange(lax.axis_size(("gx", "gy")) * BX // BX)
    blocks = jax.vmap(lambda target: owner_block(padded, target, lanes_y, corner, shift_z, window))(
        targets
    )
    canvas = lax.psum_scatter(
        blocks.reshape(lax.axis_size(("gx", "gy")) * BX, BY, padded.shape[2], window),
        ("gx", "gy"),
        scatter_dimension=0,
        tiled=True,
    )
    return finish(canvas, weight_sum)


def solution(mesh):
    return jax.shard_map(
        per_device,
        mesh=mesh,
        in_specs=(P("gx", "gy", "gz", None, None), P(), P()),
        out_specs=P("gx", "gy", None, "gz"),
        check_vma=False,
    )
```

profile of v0, /device:TPU:1, one launch (start us, length us, event | category | flops | bytes accessed | tf_op | source)
XLA Modules:
  0.0 503.3 jit_solution(18409186507023527455)
XLA Ops:
  6.5 1.3 dynamic_slice.6
  10.4 1.4 fusion.72
  12.4 6.1 %reshape.309 = f32[24,48,3,144]{3,2,1,0:T(4,128)} reshape(bf16[1,1,1,24,20736]{4,3,2,1,0:T(8,128)(2,1)} %param.3) | data formatting | bytes 2985984 | tf_op jit(solution)/shard_map/convert_element_type | solution.py:99
  18.5 1.4 compare_select_fusion
  20.2 3.8 broadcast_multiply_fusion
  24.0 12.1 %pad.12 = f32[40,112,3,192]{3,2,1,0:T(4,128)} pad(f32[24,48,3,144]{3,2,1,0:T(4,128)S(1)} %broadcast_multiply_fusion, f32[]{:T(128)} %constant.110.clone.1), padding=8_8x32_32x0_0x16_32 | pad | bytes 12312580 | tf_op jit(solution)/shard_map/jit(_pad)/pad | solution.py:65
  36.2 170.9 %while.1 = (s32[]{:T(128)}, f32[40,112,3,192]{3,2,1,0:T(4,128)}, s32[32,4]{0,1:T(4,128)S(1)}, f32[32,8,32,3,160]{4,2,3,1,0:T(8,128)}, s32[]{:T(128)}) while((s32[]{:T(128)}, f32[40,112,3,192]{3,2,1,0:T(4,128)}, s32[32,4]{0,1:T(4,128)S(1)}, f32[32,8,32,3,160]{4,2,3,1,0:T(8,128)}, s32[]{:T(128)}) %tuple.27), condition=%wide.while_cond, body=%wide.while_body.sunk | while | flops 2 | bytes 2261637 | solution.py:72
  36.8 3.7 dynamic-slice_bitcast_fusion.2
  42.2 3.7 dynamic-slice_bitcast_fusion.2
  45.8 1.0 copy_dynamic-update-slice_fusion.2
  47.5 3.7 dynamic-slice_bitcast_fusion.2
  51.2 1.0 copy_dynamic-update-slice_fusion.2
  52.9 3.7 dynamic-slice_bitcast_fusion.2
  58.2 3.7 dynamic-slice_bitcast_fusion.2
  63.5 3.7 dynamic-slice_bitcast_fusion.2
  67.2 1.0 copy_dynamic-update-slice_fusion.2
  68.8 3.7 dynamic-slice_bitcast_fusion.2
  72.5 1.0 copy_dynamic-update-slice_fusion.2
  74.2 3.7 dynamic-slice_bitcast_fusion.2
  77.8 1.1 copy_dynamic-update-slice_fusion.2
  79.5 3.7 dynamic-slice_bitcast_fusion.2
  84.9 3.7 dynamic-slice_bitcast_fusion.2
  90.2 3.7 dynamic-slice_bitcast_fusion.2
  93.8 1.1 copy_dynamic-update-slice_fusion.2
  95.6 3.7 dynamic-slice_bitcast_fusion.2
  99.2 1.1 copy_dynamic-update-slice_fusion.2
  101.0 3.7 dynamic-slice_bitcast_fusion.2
  106.3 3.7 dynamic-slice_bitcast_fusion.2
  109.9 1.0 copy_dynamic-update-slice_fusion.2
  111.6 3.7 dynamic-slice_bitcast_fusion.2
  117.0 3.7 dynamic-slice_bitcast_fusion.2
  120.6 1.0 copy_dynamic-update-slice_fusion.2
  122.3 3.7 dynamic-slice_bitcast_fusion.2
  125.9 1.1 copy_dynamic-update-slice_fusion.2
  127.7 3.7 dynamic-slice_bitcast_fusion.2
  133.0 3.7 dynamic-slice_bitcast_fusion.2
  136.6 1.1 copy_dynamic-update-slice_fusion.2
  138.3 3.7 dynamic-slice_bitcast_fusion.2
  142.0 1.1 copy_dynamic-update-slice_fusion.2
  143.7 3.7 dynamic-slice_bitcast_fusion.2
  147.3 1.1 copy_dynamic-update-slice_fusion.2
  149.0 3.7 dynamic-slice_bitcast_fusion.2
  152.7 1.1 copy_dynamic-update-slice_fusion.2
  154.4 3.7 dynamic-slice_bitcast_fusion.2
  159.7 3.7 dynamic-slice_bitcast_fusion.2
  165.0 3.7 dynamic-slice_bitcast_fusion.2
  168.7 1.1 copy_dynamic-update-slice_fusion.2
  170.4 3.7 dynamic-slice_bitcast_fusion.2
  175.7 3.7 dynamic-slice_bitcast_fusion.2
  181.0 3.7 dynamic-slice_bitcast_fusion.2
  186.4 3.7 dynamic-slice_bitcast_fusion.2
  190.0 1.1 copy_dynamic-update-slice_fusion.2
  191.7 3.7 dynamic-slice_bitcast_fusion.2
  195.4 1.1 copy_dynamic-update-slice_fusion.2
  197.1 3.7 dynamic-slice_bitcast_fusion.2
  202.4 3.7 dynamic-slice_bitcast_fusion.2
  206.1 1.1 copy_dynamic-update-slice_fusion.2
  208.3 268.0 %reduce-scatter.2.cloned.1.call-done = f32[8,32,3,160]{3,1,2,0:T(8,128)} async-done(((f32[256,32,3,160]{3,1,2,0:T(8,128)}), f32[8,32,3,160]{3,1,2,0:T(8,128)}) %reduce-scatter.2.cloned.1.call-update) | async-done | bytes 491536 | tf_op jit(solution)/shard_map/reduce_scatter | solution.py:105
  476.3 1.3 fusion.71
  477.6 7.4 %collective-permute-start = (f32[8,32,3,16]{3,1,2,0:T(8,128)S(1)}, f32[8,32,3,16]{3,1,2,0:T(8,128)S(1)}, u32[]{:S(2)}, u32[]{:S(2)}) collective-permute-start(f32[8,32,3,16]{3,1,2,0:T(8,128)S(1)} %get-tuple-element.26), channel_id=1, source_target_pairs={{0,1},{1,2},{2,3},{3,4},{4,5},{5,6},{6,7},{8,9},{9,10},{10,11},{11... | collective-permute-start | bytes 147464 | tf_op jit(solution)/shard_map/ppermute | solution.py:23
  485.0 1.9 collective-permute-start.1
  487.5 2.3 collective-permute-done
  489.7 4.4 collective-permute-done.1
  494.1 1.4 fusion.68
  (102 shorter events, 37.9 us)
Async XLA Ops:
  6.5 469.8 %reduce-scatter.2.cloned.1.call-start = ((), (), s32[]{:S(2)}) async-start(), calls=%async_computation.1 | async-start | bytes 25952256 | tf_op jit(solution)/shard_map/reduce_scatter | solution.py:105
  207.1 0.8 copy-start
  477.6 12.1 %collective-permute-start = (f32[8,32,3,16]{3,1,2,0:T(8,128)S(1)}, f32[8,32,3,16]{3,1,2,0:T(8,128)S(1)}, u32[]{:S(2)}, u32[]{:S(2)}) collective-permute-start(f32[8,32,3,16]{3,1,2,0:T(8,128)S(1)} %get-tuple-element.26), channel_id=1, source_target_pairs={{0,1},{1,2},{2,3},{3,4},{4,5},{5,6},{6,7},{8,9},{9,10},{10,11},{11... | collective-permute-start | bytes 147464 | tf_op jit(solution)/shard_map/ppermute | solution.py:23
  485.0 9.1 %collective-permute-start.1 = (f32[8,32,3,16]{3,1,2,0:T(8,128)S(1)}, f32[8,32,3,16]{3,1,2,0:T(8,128)S(1)}, u32[]{:S(2)}, u32[]{:S(2)}) collective-permute-start(f32[8,32,3,16]{3,1,2,0:T(8,128)S(1)} %get-tuple-element.27), channel_id=1, source_target_pairs={{1,0},{2,1},{3,2},{4,3},{5,4},{6,5},{7,6},{9,8},{10,9},{11,10},{12... | collective-permute-start | bytes 147464 | tf_op jit(solution)/shard_map/ppermute | solution.py:24
Sparse Core Ops, SparseCore 0:
  207.3 268.9 reduce-scatter.1
where the time goes:
time: 506 us; the launch traced here: 503 us
  waiting for transfers between devices  275 us (54%)
  local copies, waits for them, and re-layouts  194 us (38%)
  between operations  16.6 us (3%)
  starting transfers between devices  9.36 us (2%)
  other arithmetic  8.06 us (2%)
    reduce_scatter x1, waiting for transfers between devices, per_device(): lax.psum_scatter(blocks.reshape(lax.axis_size(('gx', 'gy')) * BX, BY, pad...  268 us
    gather x128, local copies, waits for them, and re-layouts  171 us
    pad x1, local copies, waits for them, and re-layouts, pad_patch(): return jnp.pad(source, ((BX, BX), (BY, BY), (0, 0), (margin, 2 * margin)))  12.1 us
  transfers between devices with their start and end apart: 3, of which 3 were waited for; matrix products, arithmetic and copies ran while one was open for 0% of the time, Pallas kernels for 0%

commit v1 on v0

v1 whole, which is shorter than its diff:
```python
import functools

import jax
import jax.numpy as jnp
from jax import lax
from jax.experimental import pallas as pl
from jax.experimental.pallas import tpu as pltpu
from jax.sharding import PartitionSpec as P

CLASSES = 3
BX, BY, BZ = 8, 32, 128
PX, PY, PZ = 24, 48, 144
GX, GY, GZ = 8, 4, 8
ROW = CLASSES * PZ
RES = 16
VROWS = PY // RES
PIECE = 1408
SLOTS = 16
F32 = jnp.float32
MESH = pl.DeviceIdType.MESH


def profile(offsets, length):
    inside = (offsets >= 0) & (offsets < length)
    centre = (length - 1) / 2.0
    spread = length / 4.0
    values = jnp.exp(-((offsets.astype(F32) - centre) ** 2) / (2.0 * spread * spread))
    return jnp.where(inside, values, 0.0)


def place():
    return lax.axis_index("gx"), lax.axis_index("gy"), lax.axis_index("gz")


def hop_of(step, lane):
    return (0, 1, 2 - 4 * (lane % 2), -1)[step]


def cut_kernel(owner_ref, start_ref, x_ref, out_ref):
    a, b, k = place()
    code = owner_ref[a, b, k]
    sy = start_ref[code // GY, code % GY, k * 3 + 1]
    lane = lax.broadcasted_iota(jnp.int32, (PX, 128), 1)
    for rho in range(RES):
        slot = lax.rem(sy + rho, RES)
        parts = []
        for v in range(VROWS):
            src = ROW * (rho + RES * v)
            base, rest = src // 128 * 128, src % 128
            width = -(-(rest + ROW) // 128) * 128
            seg = x_ref[:, base : base + width].astype(F32)
            if width < 640:
                seg = jnp.concatenate([seg, jnp.zeros((PX, 640 - width), F32)], axis=1)
            shift = (ROW * v % 128 - rest) % 640
            parts.append(pltpu.roll(seg, shift, 1) if shift else seg)
        r0, r1, r2 = parts
        seam0 = jnp.where(lane < 48, r0[:, 384:512], r1[:, 0:128])
        seam1 = jnp.where(lane < 96, r1[:, 384:512], r2[:, 0:128])
        out_ref[slot, :, 0:384] = r0[:, 0:384].astype(jnp.bfloat16)
        out_ref[slot, :, 384:512] = seam0.astype(jnp.bfloat16)
        out_ref[slot, :, 512:768] = r1[:, 128:384].astype(jnp.bfloat16)
        out_ref[slot, :, 768:896] = seam1.astype(jnp.bfloat16)
        out_ref[slot, :, 896:1408] = r2[:, 128:640].astype(jnp.bfloat16)


def cut(owner, start, x):
    return pl.pallas_call(
        cut_kernel,
        out_shape=jax.ShapeDtypeStruct((RES, PX, PIECE), jnp.bfloat16),
        in_specs=[
            pl.BlockSpec(memory_space=pltpu.SMEM),
            pl.BlockSpec(memory_space=pltpu.SMEM),
            pl.BlockSpec(memory_space=pltpu.VMEM),
        ],
        out_specs=pl.BlockSpec(memory_space=pltpu.VMEM),
    )(owner, start, x)


def greet(partners):
    barrier = pltpu.get_barrier_semaphore()
    for partner in partners:
        pl.semaphore_signal(barrier, inc=1, device_id=partner, device_id_type=MESH)
    pl.semaphore_wait(barrier, len(partners))


def scatter_kernel(x_ref, out_ref, send_sem, recv_sem, local_sem):
    a, b, k = place()
    greet(
        [
            (lax.rem(a + dz + GX, GX), lax.rem(b + db, GY), k)
            for dz in (0, 1, -1, 2, -2)
            for db in range(GY)
            if dz or db
        ]
    )
    copies = []
    for step in (2, 1, 3, 0):
        group = lax.rem(a + step, 4)
        for turn in range(GY):
            if step == 0 and turn == 0:
                continue
            to_b = lax.rem(b + turn, GY)
            if step == 2:
                hop = 2 - 4 * lax.rem(to_b, 2)
            else:
                hop = hop_of(step, 0)
            copy = pltpu.make_async_remote_copy(
                src_ref=x_ref.at[4 * group + to_b],
                dst_ref=out_ref.at[4 * step + b],
                send_sem=send_sem.at[4 * step + turn],
                recv_sem=recv_sem.at[4 * step + turn],
                device_id=(lax.rem(a + hop + GX, GX), to_b, k),
                device_id_type=MESH,
            )
            copy.start()
            copies.append(copy)
    own = pltpu.make_async_copy(x_ref.at[4 * lax.rem(a, 4) + b], out_ref.at[b], local_sem)
    own.start()
    own.wait()
    for copy in copies:
        copy.wait()


def scatter(pieces):
    return pl.pallas_call(
        scatter_kernel,
        out_shape=jax.ShapeDtypeStruct((SLOTS, PX, PIECE), jnp.bfloat16),
        in_specs=[pl.BlockSpec(memory_space=pl.ANY)],
        out_specs=pl.BlockSpec(memory_space=pl.ANY),
        scratch_shapes=[
            pltpu.SemaphoreType.DMA((SLOTS,)),
            pltpu.SemaphoreType.DMA((SLOTS,)),
            pltpu.SemaphoreType.DMA,
        ],
        compiler_params=pltpu.CompilerParams(collective_id=0, has_side_effects=True),
    )(pieces)


def blend_kernel(owner_ref, start_ref, lanes_ref, x_ref, main_ref, rim_ref, sum_ref, acc, edge):
    a, b, k = place()
    acc[...] = jnp.zeros_like(acc)
    edge[...] = jnp.zeros_like(edge)
    residue = 4 * lax.rem(a, 4) + b
    col = lax.broadcasted_iota(jnp.int32, (PX, 256), 1)
    col = jnp.where(col < 192, col, col - 256)
    along_x = profile(lax.broadcasted_iota(jnp.int32, (PX, 256), 0), PX)
    odd = 2 - 4 * lax.rem(b, 2)

    def add_patch(slot, carry):
        step = slot // 4
        hop = jnp.where(step == 2, odd, jnp.where(step == 3, -1, step))
        from_a = lax.rem(a - hop + GX, GX)
        code = owner_ref[from_a, lax.rem(slot, 4), k]
        i, j = code // GY, lax.rem(code, GY)
        sx = start_ref[i, j, k * 3]
        sy = start_ref[i, j, k * 3 + 1]
        shift_z = start_ref[i, j, k * 3 + 2] - k * BZ
        rho = lax.rem(residue - sy + 8 * RES, RES)
        first_y = (sy + rho) // RES
        along_z = profile(col - shift_z, PZ)
        for v in range(VROWS):
            along_y = profile(jnp.full((PX, 256), rho + RES * v, jnp.int32), PY)
            weight = along_x * along_y * along_z
            rolled = []
            for c in range(CLASSES):
                m = CLASSES * v + c
                base = 128 * m if m < 8 else 1152
                turn = lax.rem(shift_z - (PZ * m - base) + 512, 256)
                seg = x_ref[slot, :, base : base + 256].astype(F32)
                rolled.append(pltpu.roll(seg, turn, 1))
            for d in range(2):
                value = (rolled[d + 1] - rolled[0]) * weight
                rows = pl.ds(sx, PX)
                acc[2 * (first_y + v) + d, rows, :] += value[:, 0:128]
                edge[2 * (first_y + v) + d, rows, :] += value[:, 128:256]
        return carry

    lax.fori_loop(0, SLOTS, add_patch, 0)

    for row in range(8):
        for d in range(2):
            for block in range(8):
                main_ref[block, row // 2, row % 2, d] = acc[2 * row + d, 8 * block : 8 * block + 8, :]
    lane = lax.broadcasted_iota(jnp.int32, (64, 128), 1)
    for d in range(2):
        up = jnp.zeros((64, 128), F32)
        low = jnp.zeros((64, 128), F32)
        for row in range(8):
            value = edge[2 * row + d]
            mine = lane // 16 == row
            turned = pltpu.roll(value, 16 * row, 1) if row else value
            up = jnp.where(mine, turned, up)
            turned = pltpu.roll(value, (16 * row + 16) % 128, 1) if row < 7 else value
            low = jnp.where(mine, turned, low)
        rim_ref[0, d] = up
        rim_ref[1, d] = low

    row = lax.broadcasted_iota(jnp.int32, (BX * BY, GX * GY * GZ), 0)
    plane = profile(a * BX + lax.rem(row, BX) - lanes_ref[0:1, :], PX)
    plane = plane * profile(b * BY + row // BX - lanes_ref[1:2, :], PY)
    row = lax.broadcasted_iota(jnp.int32, (BZ, GX * GY * GZ), 0)
    depth = profile(k * BZ + row - lanes_ref[2:3, :], PZ)
    sum_ref[...] = lax.dot_general(
        plane, depth, (((1,), (1,)), ((), ())), precision=lax.Precision.HIGHEST, preferred_element_type=F32
    )


def blend(owner, start, lanes, pieces):
    return pl.pallas_call(
        blend_kernel,
        out_shape=(
            jax.ShapeDtypeStruct((8, 4, 2, 2, 8, 128), F32),
            jax.ShapeDtypeStruct((2, 2, 64, 128), F32),
            jax.ShapeDtypeStruct((BX * BY, BZ), F32),
        ),
        in_specs=[
            pl.BlockSpec(memory_space=pltpu.SMEM),
            pl.BlockSpec(memory_space=pltpu.SMEM),
            pl.BlockSpec(memory_space=pltpu.VMEM),
            pl.BlockSpec(memory_space=pltpu.VMEM),
        ],
        out_specs=(pl.BlockSpec(memory_space=pltpu.VMEM),) * 3,
        scratch_shapes=[pltpu.VMEM((16, 64, 128), F32), pltpu.VMEM((16, 64, 128), F32)],
    )(owner, start, lanes, pieces)


def gather_kernel(main_ref, rim_ref, sum_ref, out_ref, total, rims, parts, send_sem, recv_sem, rim_send, rim_recv):
    a, b, k = place()
    above, below = lax.rem(k + 1, GZ), lax.rem(k + GZ - 1, GZ)
    others = [(dz, db) for dz in (4, 3, 5, 2, 6, 1, 7, 0) for db in range(GY) if dz or db]
    partners = [(lax.rem(a + dz, GX), lax.rem(b + db, GY), k) for dz, db in others]
    greet([(a, b, above), (a, b, below)] + partners)
    rim_copies = []
    for side, to_k in ((0, above), (1, below)):
        copy = pltpu.make_async_remote_copy(
            src_ref=rim_ref.at[side],
            dst_ref=rims.at[side],
            send_sem=rim_send.at[side],
            recv_sem=rim_recv.at[side],
            device_id=(a, b, to_k),
            device_id_type=MESH,
        )
        copy.start()
        rim_copies.append(copy)
    for copy in rim_copies:
        copy.wait()
    lane = lax.broadcasted_iota(jnp.int32, (8, 128), 1)
    for block in range(8):
        for d in range(2):
            up = rims[0, d, 8 * block : 8 * block + 8, :]
            low = rims[1, d, 8 * block : 8 * block + 8, :]
            for row in range(8):
                shifted = jnp.where(lane < 16, pltpu.roll(up, (128 - 16 * row) % 128, 1), 0.0)
                shifted = shifted + jnp.where(lane >= 112, pltpu.roll(low, 112 - 16 * row, 1), 0.0)
                total[block, row // 2, row % 2, d] = main_ref[block, row // 2, row % 2, d] + shifted
    copies = []
    for at, ((dz, db), partner) in enumerate(zip(others, partners)):
        copy = pltpu.make_async_remote_copy(
            src_ref=total.at[partner[0], partner[1]],
            dst_ref=parts.at[a, b],
            send_sem=send_sem.at[at],
            recv_sem=recv_sem.at[at],
            device_id=partner,
            device_id_type=MESH,
        )
        copy.start()
        copies.append(copy)
    parts[a, b] = total[a, b]
    for copy in copies:
        copy.wait()
    for residue in range(RES):
        for h in range(2):
            y = RES * h + residue
            d1 = parts[residue // 4, residue % 4, h, 0] + parts[residue // 4 + 4, residue % 4, h, 0]
            d2 = parts[residue // 4, residue % 4, h, 1] + parts[residue // 4 + 4, residue % 4, h, 1]
            norm = sum_ref[8 * y : 8 * y + 8, :]
            d1, d2 = d1 / norm, d2 / norm
            top = jnp.maximum(jnp.maximum(d1, d2), 0.0)
            e0, e1, e2 = jnp.exp(-top), jnp.exp(d1 - top), jnp.exp(d2 - top)
            scale = 1.0 / (e0 + e1 + e2)
            out_ref[y, 0] = e0 * scale
            out_ref[y, 1] = e1 * scale
            out_ref[y, 2] = e2 * scale


def gather(main, rim, weight_sum):
    return pl.pallas_call(
        gather_kernel,
        out_shape=jax.ShapeDtypeStruct((BY, CLASSES, BX, BZ), F32),
        in_specs=[pl.BlockSpec(memory_space=pltpu.VMEM)] * 3,
        out_specs=pl.BlockSpec(memory_space=pltpu.VMEM),
        scratch_shapes=[
            pltpu.VMEM((8, 4, 2, 2, 8, 128), F32),
            pltpu.VMEM((2, 2, 64, 128), F32),
            pltpu.VMEM((8, 4, 2, 2, 8, 128), F32),
            pltpu.SemaphoreType.DMA((31,)),
            pltpu.SemaphoreType.DMA((31,)),
            pltpu.SemaphoreType.DMA((2,)),
            pltpu.SemaphoreType.DMA((2,)),
        ],
        compiler_params=pltpu.CompilerParams(collective_id=1, has_side_effects=True),
    )(main, rim, weight_sum)


def per_device(patch_logits, patch_start, patch_owner):
    start = patch_start.reshape(GX, GY, GZ * 3)
    lanes = patch_start.reshape(GX * GY * GZ, 3).T
    pieces = cut(patch_owner, start, patch_logits.reshape(PX, PY * ROW))
    pieces = scatter(pieces)
    main, rim, weight_sum = blend(patch_owner, start, lanes, pieces)
    probs = gather(main, rim, weight_sum)
    return jnp.transpose(probs, (2, 0, 1, 3))


def solution(mesh):
    return jax.shard_map(
        per_device,
        mesh=mesh,
        in_specs=(P("gx", "gy", "gz", None, None), P(), P()),
        out_specs=P("gx", "gy", None, "gz"),
        check_vma=False,
    )
```

time: 506 us -> 63.1 us (0.12)
  waiting for transfers between devices: 275 us -> 0 us
  local copies, waits for them, and re-layouts: 194 us -> 4.1 us
  Pallas kernels: 0 us -> 58.7 us
  between operations: 16.6 us -> 0.04 us
  starting transfers between devices: 9.36 us -> 0 us
  other arithmetic: 8.06 us -> 0 us
    reduce_scatter x1 -> x0, waiting for transfers between devices: 268 us -> none  [per_device(): lax.psum_scatter(blocks.reshape(lax.axis_size(('gx', 'gy')) * BX, BY, pad...]
    gather x128 -> x0, local copies, waits for them, and re-layouts: 171 us -> none
    pallas_call x0 -> x4, Pallas kernels: none -> 58.7 us  [the longest x1 26 us: gather(): pl.pallas_call(gather_kernel, out_shape=jax.ShapeDtypeStruct((BY, CLASSES...]
    pad x1 -> x0, local copies, waits for them, and re-layouts: 12.1 us -> none  [pad_patch(): return jnp.pad(source, ((BX, BX), (BY, BY), (0, 0), (margin, 2 * margin)))]
    ppermute x2 -> x0, starting transfers between devices: 9.36 us -> none  [the longest x1 7.44 us: extended(): before = lax.ppermute(last, axis, up)]
    ppermute x2 -> x0, waiting for transfers between devices: 6.67 us -> none  [the longest x1 4.4 us: extended(): after = lax.ppermute(first, axis, down)]
    convert_element_type x1 -> x0, local copies, waits for them, and re-layouts: 6.12 us -> none  [per_device(): blended = logits * weight]
  transfers between devices with their start and end apart: 3 -> 0, of which waited for: 3 -> 0; matrix products, arithmetic and copies ran while one was open for 0% -> 0% of each run, Pallas kernels for 0% -> 0%
where the time goes in v1:
time: 63.1 us; the launch traced here: 62.8 us
  Pallas kernels  58.7 us (93%)
  local copies, waits for them, and re-layouts  4.1 us (6%)
    pallas_call x1, Pallas kernels, gather(): pl.pallas_call(gather_kernel, out_shape=jax.ShapeDtypeStruct((BY, CLASSES...  26 us
    pallas_call x1, Pallas kernels, scatter(): pl.pallas_call(scatter_kernel, out_shape=jax.ShapeDtypeStruct((SLOTS, PX,...  25 us
    pallas_call x1, Pallas kernels, blend(): pl.pallas_call(blend_kernel, out_shape=(jax.ShapeDtypeStruct((8, 4, 2, 2,...  5.06 us
    pallas_call x1, Pallas kernels, cut(): pl.pallas_call(cut_kernel, out_shape=jax.ShapeDtypeStruct((RES, PX, PIECE...  2.62 us
    transpose x1, local copies, waits for them, and re-layouts, per_device(): return jnp.transpose(probs, (2, 0, 1, 3))  1.82 us

profile of v1, /device:TPU:1, one launch (start us, length us, event | category | flops | bytes accessed | tf_op | source)
XLA Modules:
  0.0 62.8 jit_solution(10695421092795528464)
XLA Ops:
  0.0 0.9 %copy.7 = s32[8,4,8,3]{0,1,3,2:T(4,128)S(1)} copy(s32[8,4,8,3]{2,1,3,0:T(4,128)} %param.4) | data formatting | bytes 6144 | tf_op args[1]
  0.9 0.7 %copy.10.start_ref = s32[8,4,24]{2,1,0:T(4,128)} copy(s32[8,4,24]{0,1,2:T(4,128)S(1)} %bitcast.8) | data formatting | bytes 6144 | tf_op jit(solution)/shard_map/reshape | solution.py:306
  1.6 2.6 %shard_map.37.x_ref = bf16[16,24,1408]{2,1,0:T(8,128)(2,1)} custom-call(s32[8,4,8]{2,1,0:T(4,128)} %owner_ref.3, s32[8,4,24]{2,1,0:T(4,128)} %copy.10.start_ref, bf16[24,20736]{1,0:T(8,128)(2,1)} %bitcast.7), custom_call_target="tpu_custom_call" | custom-call | tf_op jit(solution)/shard_map/pallas_call | solution.py:67
  4.2 0.0 copy-start
  4.2 25.0 %shard_map.38.x_ref = bf16[16,24,1408]{2,1,0:T(8,128)(2,1)} custom-call(bf16[16,24,1408]{2,1,0:T(8,128)(2,1)} %shard_map.37.x_ref), custom_call_target="tpu_custom_call" | custom-call | tf_op jit(solution)/shard_map/pallas_call | solution.py:125
  29.2 0.0 copy-done
  29.2 0.7 %reshape.10 = s32[256,3]{0,1:T(4,128)} reshape(s32[8,4,8,3]{2,1,0,3:T(4,128)S(1)} %copy.8) | data formatting | bytes 6144 | tf_op jit(solution)/shard_map/reshape | solution.py:307
  29.9 5.1 %shard_map.39 = (f32[8,4,2,2,8,128]{5,4,3,2,1,0:T(8,128)}, f32[2,2,64,128]{3,2,1,0:T(8,128)}, f32[256,128]{1,0:T(8,128)}) custom-call(s32[8,4,8]{2,1,0:T(4,128)} %owner_ref.3, s32[8,4,24]{2,1,0:T(4,128)} %copy.10.start_ref, s32[3,256]{1,0:T(4,128)} %bitcast.9, bf16[16,24,1408]{2,1,0:T(8,128)(2,1)} %shard_map.38.x_ref), custom_call_target="tpu_custom_call" | custom-call | tf_op jit(solution)/shard_map/pallas_call | solution.py:209
  35.0 26.0 %shard_map.40 = f32[32,3,8,128]{3,2,1,0:T(8,128)} custom-call(f32[8,4,2,2,8,128]{5,4,3,2,1,0:T(8,128)} %get-tuple-element.8.main_ref, f32[2,2,64,128]{3,2,1,0:T(8,128)} %get-tuple-element.9.rim_ref, f32[256,128]{1,0:T(8,128)} %get-tuple-element.10.sum_ref), custom_call_target="tpu_custom_call" | custom-call | tf_op jit(solution)/shard_map/pallas_call | solution.py:287
  61.0 1.8 %copy.11 = f32[8,32,3,128]{3,1,2,0:T(8,128)} copy(f32[8,32,3,128]{3,0,2,1:T(8,128)} %bitcast.6) | data formatting | bytes 786432 | tf_op jit(solution)/shard_map/transpose | solution.py:312
  (1 shorter events, 0.0 us)
Async XLA Ops:
  4.2 25.0 %copy-start = (s32[8,4,8,3]{2,1,3,0:T(4,128)S(1)}, s32[8,4,8,3]{2,1,3,0:T(4,128)}, u32[]{:S(2)}) copy-start(s32[8,4,8,3]{2,1,3,0:T(4,128)} %param.4) | copy-start | bytes 9220

commit v2 on v0

v2 whole, which is shorter than its diff:
```python
import jax
import jax.numpy as jnp
from jax import lax
from jax.experimental import pallas as pl
from jax.experimental.pallas import tpu as pltpu
from jax.sharding import PartitionSpec as P

CLASSES = 3
BX, BY, BZ = 8, 32, 128
PX, PY, PZ = 24, 48, 144
GX, GY, GZ = 8, 4, 8
ROW = CLASSES * PZ
RES = 16
VROWS = PY // RES
GROUPS = PX // 8
TILES = 31
LAST = PY * ROW // 128 - 1
MARGIN = 40
OWNERS = GX * GY
F32 = jnp.float32
BF16 = jnp.bfloat16
MESH = pl.DeviceIdType.MESH


def profile(offsets, length):
    inside = (offsets >= 0) & (offsets < length)
    centre = (length - 1) / 2.0
    spread = length / 4.0
    values = jnp.exp(-((offsets.astype(F32) - centre) ** 2) / (2.0 * spread * spread))
    return jnp.where(inside, values, 0.0)


def iota(dim):
    return lax.broadcasted_iota(jnp.int32, (8, 128), dim)


def wrap(index, size):
    return lax.rem(index + size, size)


def hop_of(step, to_b):
    return (0, 1, 2 - 4 * lax.rem(to_b, 2), -1)[step]


def blend_kernel(
    owner_ref, start_ref, x_ref, out_ref,
    patch, send, recv, table, sums, value, acc, rim, rims, total, parts,
    in_sem, send_sem, recv_sem, rim_send, rim_recv, part_send, part_recv,
):
    a, b, k = lax.axis_index("gx"), lax.axis_index("gy"), lax.axis_index("gz")
    above, below = wrap(k + 1, GZ), wrap(k - 1, GZ)
    barrier = pltpu.get_barrier_semaphore()
    for dz in range(GX):
        for db in range(GY):
            if dz or db:
                to = (wrap(a + dz, GX), wrap(b + db, GY), k)
                pl.semaphore_signal(barrier, inc=1, device_id=to, device_id_type=MESH)
    for to_k in (above, below):
        pl.semaphore_signal(barrier, inc=1, device_id=(a, b, to_k), device_id_type=MESH)
    load = pltpu.make_async_copy(x_ref, patch, in_sem)
    load.start()

    lane, sub = iota(1), iota(0)

    def start_of(code, at_k, dim):
        return start_ref[code // GY, dim, lax.rem(code, GY), at_k]

    zero = jnp.zeros((8, 128), F32)
    for s in range(4):
        for d in range(2):
            for t in range(2):
                for v in range(VROWS):
                    for row in (*range(0, MARGIN, 8), *range(MARGIN + PX, PX + 2 * MARGIN, 8)):
                        value[s, v, d, t, row : row + 8, :] = zero
                for row in range(0, PX + 2 * MARGIN, 8):
                    value[s, VROWS, d, t, row : row + 8, :] = zero
    for offset in range(3 * PX):
        table[offset] = profile(jnp.full((8, 128), offset - PX, jnp.int32), PX)

    my_sy = start_of(owner_ref[a, b, k], k, 1)
    load.wait()

    def cut(residue, store):
        rho = lax.rem(residue - my_sy + 8 * RES, RES)
        for g in range(GROUPS):
            held = [[], [], []]
            for v in range(VROWS):
                into = ROW * v % 128
                delta = ROW * rho + ROW * RES * v - into
                first = (delta + 127) // 128
                turn = first * 128 - delta
                count = -(-(into + ROW) // 128)
                turned = []
                for t in range(-1, count):
                    at = first + t
                    if t == -1:
                        at = jnp.maximum(at, 0)
                    if t == count - 1:
                        at = jnp.minimum(at, LAST)
                    tile = patch[g, at]
                    turned.append(pltpu.roll(tile.astype(F32), turn, 1))
                held[v] = [jnp.where(lane < turn, turned[t], turned[t + 1]) for t in range(count)]
            r0, r1, r2 = held
            tiles = r0[:3] + [jnp.where(lane < 48, r0[3], r1[0])] + r1[1:3]
            tiles = tiles + [jnp.where(lane < 96, r1[3], r2[0])] + r2[1:4]
            for t in range(10):
                store(GROUPS * t + g, tiles[t].astype(BF16))
            tail = r2[4] if g == 0 else pltpu.roll(r2[4], 16 * g, 1)
            tails = tail if g == 0 else jnp.where(lane < 16 * g, tails, tail)
        store(TILES - 1, tails.astype(BF16))

    def piece_copy(step, turn):
        to_b = wrap(b + turn, GY)
        return pltpu.make_async_remote_copy(
            src_ref=send.at[4 * step + turn],
            dst_ref=recv.at[4 * step + b],
            send_sem=send_sem.at[4 * step + turn],
            recv_sem=recv_sem.at[4 * step + b],
            device_id=(wrap(a + hop_of(step, to_b), GX), to_b, k),
            device_id_type=MESH,
        )

    def piece_arrival(step, from_b):
        return pltpu.make_async_remote_copy(
            src_ref=send.at[4 * step],
            dst_ref=recv.at[4 * step + from_b],
            send_sem=send_sem.at[4 * step],
            recv_sem=recv_sem.at[4 * step + from_b],
            device_id=(a, b, above),
            device_id_type=MESH,
        )

    for step in (2, 1, 3, 0):

        def cut_one(turn, carry, step=step):
            residue = 4 * lax.rem(a + step, 4) + wrap(b + turn, GY)

            def store(tile, what):
                send[4 * step + turn, tile] = what

            cut(residue, store)
            return carry

        lax.fori_loop(1 if step == 0 else 0, GY, cut_one, 0)
        if step == 2:
            pl.semaphore_wait(barrier, OWNERS + 1)
        for turn in range(1 if step == 0 else 0, GY):
            piece_copy(step, turn).start()

    def store_own(tile, what):
        recv[b, tile] = what

    cut(4 * lax.rem(a, 4) + b, store_own)

    def add_weight(index, carry):
        i, j, at_k = a - 2 + index // 9, b - 1 + lax.rem(index // 3, 3), k - 1 + lax.rem(index, 3)
        valid = (i >= 0) & (i < GX) & (j >= 0) & (j < GY) & (at_k >= 0) & (at_k < GZ)
        i, j, at_k = jnp.clip(i, 0, GX - 1), jnp.clip(j, 0, GY - 1), jnp.clip(at_k, 0, GZ - 1)
        along_z = profile(BZ * k + lane - start_ref[i, 2, j, at_k], PZ)
        along_z = along_z * jnp.where(valid, 1.0, 0.0)
        y = BY * b + sub - start_ref[i, 1, j, at_k]
        planes = [profile(y + 8 * g, PY) * along_z for g in range(4)]
        base = jnp.clip(BX * a - start_ref[i, 0, j, at_k] + PX, 0, 2 * PX)
        new = []
        for x in range(BX):
            along_x = table[base + x]
            new += [carry[4 * x + g] + along_x * planes[g] for g in range(4)]
        return tuple(new)

    weights = lax.fori_loop(0, 45, add_weight, (zero,) * 32)
    for at in range(32):
        sums[at] = weights[at]

    residue = 4 * lax.rem(a, 4) + b
    along_x = [profile(sub + 8 * g, PX) for g in range(GROUPS)]
    columns = (lane, jnp.where(lane < 64, lane + 128, lane - 128))

    def corner(step, from_b):
        from_a = wrap(a - hop_of(step, b), GX)
        code = owner_ref[from_a, from_b, k]
        sy = start_of(code, k, 1)
        rho = lax.rem(residue - sy + 8 * RES, RES)
        return start_of(code, k, 0), (sy + rho) // RES, rho, start_of(code, k, 2) - BZ * k

    for group, step in enumerate((0, 1, 3, 2)):

        def weigh(from_b, carry, step=step):
            if step == 0:

                @pl.when(from_b != b)
                def _():
                    piece_arrival(step, from_b).wait_recv()

            else:
                piece_arrival(step, from_b).wait_recv()
            _, _, rho, shift_z = corner(step, from_b)
            along_z = [profile(c - shift_z, PZ) for c in columns]
            for v in range(VROWS):
                along_y = profile(jnp.full((8, 128), RES * v, jnp.int32) + rho, PY)
                turns, swaps = [], []
                for c in range(CLASSES):
                    m = CLASSES * v + c
                    turn = lax.rem(shift_z - 16 * (m % 8) + 512, 256)
                    low = lax.rem(turn, 128)
                    turns.append(low)
                    high = turn // 128
                    swaps.append((jnp.where(lane < low, 1, 0) + high) == 1)
                for g in range(GROUPS):
                    rolled = []
                    for c in range(CLASSES):
                        m = CLASSES * v + c
                        column = m if m < 8 else 9
                        first = recv[4 * step + from_b, GROUPS * column + g].astype(F32)
                        if column == 9:
                            second = recv[4 * step + from_b, TILES - 1].astype(F32)
                            second = pltpu.roll(second, 128 - 16 * g, 1) if g else second
                        else:
                            second = recv[4 * step + from_b, GROUPS * (column + 1) + g].astype(F32)
                        first, second = pltpu.roll(first, turns[c], 1), pltpu.roll(second, turns[c], 1)
                        rolled.append((jnp.where(swaps[c], second, first), jnp.where(swaps[c], first, second)))
                    along_xy = along_x[g] * along_y
                    rows = slice(MARGIN + 8 * g, MARGIN + 8 * g + 8)
                    for t in range(2):
                        weight = along_xy * along_z[t]
                        for d in range(2):
                            value[from_b, v, d, t, rows, :] = (rolled[d + 1][t] - rolled[0][t]) * weight
            return carry

        lax.fori_loop(0, GY, weigh, 0)
        corners = [corner(step, from_b) for from_b in range(GY)]
        for t in (1, 0):

            def place(y, carry, t=t, group=group, corners=corners):
                places = []
                for sx, first_y, _, _ in corners:
                    v = y - first_y
                    places.append((jnp.where((v >= 0) & (v < VROWS), v, VROWS), MARGIN - sx))
                for d in range(2):
                    for block in range(GX):
                        rows = slice(8 * block, 8 * block + 8)
                        got = None if group == 0 else acc[y, d, t, rows, :]
                        for s, (v, row) in enumerate(places):
                            more = value[s, v, d, t, pl.ds(row + 8 * block, 8), :]
                            got = more if got is None else got + more
                        acc[y, d, t, rows, :] = got
                return carry

            lax.fori_loop(0, 8, place, 0)
            if group == 3 and t == 1:
                for d in range(2):
                    for block in range(GX):
                        rows = slice(8 * block, 8 * block + 8)
                        up, low = zero, zero
                        for y in range(8):
                            turned = acc[y, d, 1, rows, :]
                            turned = pltpu.roll(turned, 16 * y, 1) if y else turned
                            up = jnp.where(lane // 16 == y, turned, up)
                            low = jnp.where(lane // 16 == (y + 7) % 8, turned, low)
                        rim[0, d, rows, :] = up
                        rim[1, d, rows, :] = low
                rim_copies = []
                for side, to_k in ((0, above), (1, below)):
                    copy = pltpu.make_async_remote_copy(
                        src_ref=rim.at[side],
                        dst_ref=rims.at[side],
                        send_sem=rim_send.at[side],
                        recv_sem=rim_recv.at[side],
                        device_id=(a, b, to_k),
                        device_id_type=MESH,
                    )
                    copy.start()
                    rim_copies.append(copy)
    for copy in rim_copies:
        copy.wait()

    def whom(index):
        far = index // GY
        dz = 4 + ((far + 1) // 2) * (1 - 2 * lax.rem(far, 2))
        return wrap(a + dz, GX), wrap(b + lax.rem(index + 1, GY), GY)

    def part_copy(index):
        to_a, to_b = whom(index)
        return pltpu.make_async_remote_copy(
            src_ref=total.at[pl.ds(pl.multiple_of(32 * (GY * to_a + to_b), 32), 32)],
            dst_ref=parts.at[pl.ds(pl.multiple_of(32 * (GY * a + b), 32), 32)],
            send_sem=part_send.at[index],
            recv_sem=part_recv.at[index],
            device_id=(to_a, to_b, k),
            device_id_type=MESH,
        )

    def finish_owner(to_a, to_b, store):
        rows = pl.ds(pl.multiple_of(8 * to_a, 8), 8)
        for h in range(2):
            y = 2 * to_b + h
            for d in range(2):
                up = pltpu.roll(rims[0, d, rows, :], lax.rem(128 - 16 * y, 128), 1)
                low = pltpu.roll(rims[1, d, rows, :], lax.rem(256 - 16 * y, 128), 1)
                more = jnp.where(lane < 16, up, jnp.where(lane >= 112, low, 0.0))
                store(16 * h + 8 * d, acc[y, d, 0, rows, :] + more)

    def send_part(index, carry):
        to_a, to_b = whom(index)

        def store(row, what):
            total[pl.ds(pl.multiple_of(32 * (GY * to_a + to_b) + row, 8), 8), :] = what

        finish_owner(to_a, to_b, store)

        @pl.when(index > 0)
        def _():
            part_copy(index - 1).start()

        return carry

    lax.fori_loop(0, OWNERS - 1, send_part, 0)

    def store_mine(row, what):
        parts[pl.ds(pl.multiple_of(32 * (GY * a + b) + row, 8), 8), :] = what

    finish_owner(a, b, store_mine)
    part_copy(OWNERS - 2).start()

    for step in range(4):
        for turn in range(1 if step == 0 else 0, GY):
            piece_copy(step, turn).wait_send()

    def await_part(index, carry):
        part_copy(index).wait()
        return carry

    lax.fori_loop(0, OWNERS - 1, await_part, 0)

    for x in range(BX):
        for h in range(2):
            for g in range(2):
                halves = []
                for d in range(2):
                    row = 8 * g * 32 + 16 * h + 8 * d + x
                    one = parts[pl.ds(row, 8, stride=32), :]
                    halves.append(one + parts[pl.ds(row + 512, 8, stride=32), :])
                norm = sums[4 * x + 2 * h + g]
                d1, d2 = halves[0] / norm, halves[1] / norm
                top = jnp.maximum(jnp.maximum(d1, d2), 0.0)
                e0, e1, e2 = jnp.exp(-top), jnp.exp(d1 - top), jnp.exp(d2 - top)
                scale = 1.0 / (e0 + e1 + e2)
                rows = slice(16 * h + 8 * g, 16 * h + 8 * g + 8)
                out_ref[x, 0, rows, :] = e0 * scale
                out_ref[x, 1, rows, :] = e1 * scale
                out_ref[x, 2, rows, :] = e2 * scale


def per_device(patch_logits, patch_start, patch_owner):
    tiles = patch_logits.reshape(GROUPS, 8, LAST + 1, 128)
    probs = pl.pallas_call(
        blend_kernel,
        out_shape=jax.ShapeDtypeStruct((BX, CLASSES, BY, BZ), F32),
        in_specs=[
            pl.BlockSpec(memory_space=pltpu.SMEM),
            pl.BlockSpec(memory_space=pltpu.SMEM),
            pl.BlockSpec(memory_space=pl.ANY),
        ],
        out_specs=pl.BlockSpec(memory_space=pltpu.VMEM),
        scratch_shapes=[
            pltpu.VMEM((GROUPS, LAST + 1, 8, 128), BF16),
            pltpu.VMEM((16, TILES, 8, 128), BF16),
            pltpu.VMEM((16, TILES, 8, 128), BF16),
            pltpu.VMEM((3 * PX, 8, 128), F32),
            pltpu.VMEM((32, 8, 128), F32),
            pltpu.VMEM((4, VROWS + 1, 2, 2, PX + 2 * MARGIN, 128), F32),
            pltpu.VMEM((8, 2, 2, 64, 128), F32),
            pltpu.VMEM((2, 2, 64, 128), F32),
            pltpu.VMEM((2, 2, 64, 128), F32),
            pltpu.VMEM((32 * OWNERS, 128), F32),
            pltpu.VMEM((32 * OWNERS, 128), F32),
            pltpu.SemaphoreType.DMA,
            pltpu.SemaphoreType.DMA((16,)),
            pltpu.SemaphoreType.DMA((16,)),
            pltpu.SemaphoreType.DMA((2,)),
            pltpu.SemaphoreType.DMA((2,)),
            pltpu.SemaphoreType.DMA((OWNERS,)),
            pltpu.SemaphoreType.DMA((OWNERS,)),
        ],
        compiler_params=pltpu.CompilerParams(collective_id=0, has_side_effects=True),
    )(patch_owner, jnp.transpose(patch_start, (0, 3, 1, 2)), jnp.transpose(tiles, (0, 2, 1, 3)))
    return jnp.transpose(probs, (0, 2, 1, 3))


def solution(mesh):
    return jax.shard_map(
        per_device,
        mesh=mesh,
        in_specs=(P("gx", "gy", "gz", None, None), P(), P()),
        out_specs=P("gx", "gy", None, "gz"),
        check_vma=False,
    )
```

time: 506 us -> 52.7 us (0.10)
  waiting for transfers between devices: 275 us -> 0 us
  local copies, waits for them, and re-layouts: 194 us -> 1.77 us
  Pallas kernels: 0 us -> 50.6 us
  between operations: 16.6 us -> 0.01 us
  starting transfers between devices: 9.36 us -> 0 us
  other arithmetic: 8.06 us -> 0 us
    reduce_scatter x1 -> x0, waiting for transfers between devices: 268 us -> none  [per_device(): lax.psum_scatter(blocks.reshape(lax.axis_size(('gx', 'gy')) * BX, BY, pad...]
    gather x128 -> x0, local copies, waits for them, and re-layouts: 171 us -> none
    pallas_call x0 -> x1, Pallas kernels: none -> 50.6 us  [per_device(): pl.pallas_call(blend_kernel, out_shape=jax.ShapeDtypeStruct((BX, CLASSES,...]
    pad x1 -> x0, local copies, waits for them, and re-layouts: 12.1 us -> none  [pad_patch(): return jnp.pad(source, ((BX, BX), (BY, BY), (0, 0), (margin, 2 * margin)))]
    ppermute x2 -> x0, starting transfers between devices: 9.36 us -> none  [the longest x1 7.44 us: extended(): before = lax.ppermute(last, axis, up)]
    ppermute x2 -> x0, waiting for transfers between devices: 6.67 us -> none  [the longest x1 4.4 us: extended(): after = lax.ppermute(first, axis, down)]
    convert_element_type x1 -> x0, local copies, waits for them, and re-layouts: 6.12 us -> none  [per_device(): blended = logits * weight]
  transfers between devices with their start and end apart: 3 -> 0, of which waited for: 3 -> 0; matrix products, arithmetic and copies ran while one was open for 0% -> 0% of each run, Pallas kernels for 0% -> 0%
where the time goes in v2:
time: 52.7 us; the launch traced here: 52.4 us
  Pallas kernels  50.6 us (96%)
  local copies, waits for them, and re-layouts  1.77 us (3%)
    pallas_call x1, Pallas kernels, per_device(): pl.pallas_call(blend_kernel, out_shape=jax.ShapeDtypeStruct((BX, CLASSES,...  50.6 us
    unnamed x1, local copies, waits for them, and re-layouts  1.77 us

profile of v2, /device:TPU:1, one launch (start us, length us, event | category | flops | bytes accessed | tf_op | source)
XLA Modules:
  0.0 52.4 jit_solution(14636750751287918737)
XLA Ops:
  0.0 50.6 %shard_map.37 = f32[8,3,32,128]{3,2,1,0:T(8,128)} custom-call(s32[8,4,8]{2,1,0:T(4,128)} %owner_ref.1, s32[8,3,4,8]{3,2,1,0:T(4,128)} %bitcast.7, bf16[3,162,8,128]{3,2,1,0:T(8,128)(2,1)} %bitcast.6), custom_call_target="tpu_custom_call" | custom-call | tf_op jit(solution)/shard_map/pallas_call | solution.py:355
  50.6 1.8 %copy.5 = f32[8,32,3,128]{3,1,2,0:T(8,128)} copy(f32[8,32,3,128]{3,1,2,0:T(8,128)} %bitcast.5) | data formatting | bytes 786432

commit v3 on v2

v3 whole, which is shorter than its diff:
```python
import jax
import jax.numpy as jnp
from jax import lax
from jax.experimental import pallas as pl
from jax.experimental.pallas import tpu as pltpu
from jax.sharding import PartitionSpec as P

CLASSES = 3
BX, BY, BZ = 8, 32, 128
PX, PY, PZ = 24, 48, 144
GX, GY, GZ = 8, 4, 8
ROW = CLASSES * PZ
RES = 16
VROWS = PY // RES
GROUPS = PX // 8
TILES = (21, 11)
LAST = PY * ROW // 128 - 1
MARGIN = 40
OWNERS = GX * GY
F32 = jnp.float32
BF16 = jnp.bfloat16
MESH = pl.DeviceIdType.MESH


def profile(offsets, length):
    inside = (offsets >= 0) & (offsets < length)
    centre = (length - 1) / 2.0
    spread = length / 4.0
    values = jnp.exp(-((offsets.astype(F32) - centre) ** 2) / (2.0 * spread * spread))
    return jnp.where(inside, values, 0.0)


def iota(dim):
    return lax.broadcasted_iota(jnp.int32, (8, 128), dim)


def wrap(index, size):
    return lax.rem(index + size, size)


def hop_of(step, to_b):
    return (0, 1, 2 - 4 * lax.rem(to_b, 2), -1)[step]


def blend_kernel(
    owner_ref, start_ref, x_ref, out_ref,
    patch, send0, send1, recv0, recv1, table, sums, kept, value, acc, rim, rims, total, parts,
    in_sem, send_sem, recv_sem, rim_send, rim_recv, part_send, part_recv,
):
    a, b, k = lax.axis_index("gx"), lax.axis_index("gy"), lax.axis_index("gz")
    above, below = wrap(k + 1, GZ), wrap(k - 1, GZ)
    send, recv = (send0, send1), (recv0, recv1)
    near = [
        (wrap(a + dz, GX), wrap(b + db, GY), k) for dz in (0, 1, -1, 2, -2) for db in range(GY) if dz or db
    ] + [(a, b, above), (a, b, below)]
    barrier = pltpu.get_barrier_semaphore()
    for to in near:
        pl.semaphore_signal(barrier, inc=1, device_id=to, device_id_type=MESH)
    load = pltpu.make_async_copy(x_ref, patch, in_sem)
    load.start()

    lane, sub = iota(1), iota(0)
    zero = jnp.zeros((8, 128), F32)

    def start_of(code, at_k, dim):
        return start_ref[code // GY, dim, lax.rem(code, GY), at_k]

    my_sy = start_of(owner_ref[a, b, k], k, 1)
    load.wait()

    def cut(residue, store):
        rho = lax.rem(residue - my_sy + 8 * RES, RES)
        for half, (skip, length) in enumerate(((0, 2 * PZ), (2 * PZ, PZ))):
            for g in range(GROUPS):
                tiles = {}
                for v in range(VROWS):
                    into = length * v
                    delta = ROW * rho + (ROW * RES * v + skip - into)
                    first = (delta + 127) // 128
                    turn = first * 128 - delta
                    low, high = into // 128, (into + length - 1) // 128
                    turned = []
                    for t in range(low - 1, high + 1):
                        at = first + t
                        if t < 0:
                            at = jnp.maximum(at, 0)
                        if half == 1 and v == VROWS - 1 and t == high:
                            at = jnp.minimum(at, LAST)
                        turned.append(pltpu.roll(patch[g, at].astype(F32), turn, 1))
                    for t in range(low, high + 1):
                        tile = jnp.where(lane < turn, turned[t - low], turned[t - low + 1])
                        tiles[t] = jnp.where(lane < into % 128, tiles[t], tile) if t in tiles else tile
                for t in range(7 if half == 0 else 3):
                    store(half, GROUPS * t + g, tiles[t].astype(BF16))
                if half == 1:
                    if g == 0:
                        tail = tiles[3]
                    elif g == 1:
                        store(1, 9, jnp.where(lane < 48, tail, pltpu.roll(tiles[3], 48, 1)).astype(BF16))
                    else:
                        store(1, 10, tiles[3].astype(BF16))

    def piece_copy(half, step, turn):
        to_b = wrap(b + turn, GY)
        return pltpu.make_async_remote_copy(
            src_ref=send[half].at[4 * step + turn],
            dst_ref=recv[half].at[4 * step + b],
            send_sem=send_sem.at[half, 4 * step + turn],
            recv_sem=recv_sem.at[half, 4 * step + b],
            device_id=(wrap(a + hop_of(step, to_b), GX), to_b, k),
            device_id_type=MESH,
        )

    def piece_arrival(half, step, from_b):
        return pltpu.make_async_remote_copy(
            src_ref=send[half].at[4 * step],
            dst_ref=recv[half].at[4 * step + from_b],
            send_sem=send_sem.at[half, 4 * step],
            recv_sem=recv_sem.at[half, 4 * step + from_b],
            device_id=(a, b, above),
            device_id_type=MESH,
        )

    turns_of = ((2, range(GY)), (1, range(GY)), (3, range(GY)), (0, range(1, GY)))
    for step, turns in turns_of:

        def cut_one(turn, carry, step=step):
            residue = 4 * lax.rem(a + step, 4) + wrap(b + turn, GY)

            def store(half, tile, what):
                send[half][4 * step + turn, tile] = what

            cut(residue, store)
            return carry

        lax.fori_loop(turns.start, GY, cut_one, 0)
        if step == 2:
            pl.semaphore_wait(barrier, len(near))
        for turn in turns:
            piece_copy(0, step, turn).start()
    for step, turns in turns_of:
        for turn in turns:
            piece_copy(1, step, turn).start()

    def store_own(half, tile, what):
        recv[half][b, tile] = what

    cut(4 * lax.rem(a, 4) + b, store_own)

    for s in range(4):
        for t in range(2):
            for v in range(VROWS):
                for row in (*range(0, MARGIN, 8), *range(MARGIN + PX, PX + 2 * MARGIN, 8)):
                    value[s, v, t, row : row + 8, :] = zero
            for row in range(0, PX + 2 * MARGIN, 8):
                value[s, VROWS, t, row : row + 8, :] = zero
    for offset in range(3 * PX):
        table[offset] = profile(jnp.full((8, 128), offset - PX, jnp.int32), PX)

    def add_weight(index, carry):
        i, j, at_k = a - 2 + index // 9, b - 1 + lax.rem(index // 3, 3), k - 1 + lax.rem(index, 3)
        valid = (i >= 0) & (i < GX) & (j >= 0) & (j < GY) & (at_k >= 0) & (at_k < GZ)
        i, j, at_k = jnp.clip(i, 0, GX - 1), jnp.clip(j, 0, GY - 1), jnp.clip(at_k, 0, GZ - 1)
        along_z = profile(BZ * k + lane - start_ref[i, 2, j, at_k], PZ)
        along_z = along_z * jnp.where(valid, 1.0, 0.0)
        y = BY * b + sub - start_ref[i, 1, j, at_k]
        planes = [profile(y + 8 * g, PY) * along_z for g in range(4)]
        base = jnp.clip(BX * a - start_ref[i, 0, j, at_k] + PX, 0, 2 * PX)
        new = []
        for x in range(BX):
            along_x = table[base + x]
            new += [carry[4 * x + g] + along_x * planes[g] for g in range(4)]
        return tuple(new)

    weights = lax.fori_loop(0, 45, add_weight, (zero,) * 32)
    for at in range(32):
        sums[at] = weights[at]

    residue = 4 * lax.rem(a, 4) + b
    along_x = [profile(sub + 8 * g, PX) for g in range(GROUPS)]
    columns = (lane, jnp.where(lane < 64, lane + 128, lane - 128))

    def corner(step, from_b):
        from_a = wrap(a - hop_of(step, b), GX)
        code = owner_ref[from_a, from_b, k]
        sy = start_of(code, k, 1)
        rho = lax.rem(residue - sy + 8 * RES, RES)
        return start_of(code, k, 0), (sy + rho) // RES, rho, start_of(code, k, 2) - BZ * k

    def aligned(first, second, shift, lead):
        turn = lax.rem(shift - lead + 512, 256)
        low = lax.rem(turn, 128)
        swap = (jnp.where(lane < low, 1, 0) + turn // 128) == 1
        first, second = pltpu.roll(first.astype(F32), low, 1), pltpu.roll(second.astype(F32), low, 1)
        return jnp.where(swap, second, first), jnp.where(swap, first, second)

    def weigh_group(half, step):
        def weigh(from_b, carry):
            slot = 4 * step + from_b
            if step == 0:

                @pl.when(from_b != b)
                def _():
                    piece_arrival(half, step, from_b).wait_recv()

            else:
                piece_arrival(half, step, from_b).wait_recv()
            _, _, rho, shift = corner(step, from_b)
            along_z = [profile(c - shift, PZ) for c in columns]
            for v in range(VROWS):
                along_y = profile(jnp.full((8, 128), RES * v, jnp.int32) + rho, PY)
                for g in range(GROUPS):
                    if half == 0:
                        pair = []
                        for m in (2 * v, 2 * v + 1):
                            ends = recv0[slot, GROUPS * m + g], recv0[slot, GROUPS * m + GROUPS + g]
                            pair.append(aligned(*ends, shift, 16 * m))
                        base, upper = pair
                        for t in range(2):
                            kept[slot, v, t, g] = base[t]
                    else:
                        first = recv1[slot, GROUPS * v + g].astype(F32)
                        if v < VROWS - 1:
                            second = recv1[slot, GROUPS * v + GROUPS + g].astype(F32)
                        else:
                            second = recv1[slot, 9 + g // 2].astype(F32)
                            second = pltpu.roll(second, 80, 1) if g == 1 else second
                        upper = aligned(first, second, shift, 16 * v)
                        base = [kept[slot, v, t, g] for t in range(2)]
                    along_xy = along_x[g] * along_y
                    rows = slice(MARGIN + 8 * g, MARGIN + 8 * g + 8)
                    for t in range(2):
                        value[from_b, v, t, rows, :] = (upper[t] - base[t]) * (along_xy * along_z[t])
            return carry

        lax.fori_loop(0, GY, weigh, 0)

    def place_group(half, step, t, first):
        corners = [corner(step, from_b) for from_b in range(GY)]

        def place(y, carry):
            places = []
            for sx, first_y, _, _ in corners:
                v = y - first_y
                places.append((jnp.where((v >= 0) & (v < VROWS), v, VROWS), MARGIN - sx))
            for block in range(GX):
                rows = slice(8 * block, 8 * block + 8)
                got = None if first else acc[half, y, t, rows, :]
                for s, (v, row) in enumerate(places):
                    more = value[s, v, t, pl.ds(row + 8 * block, 8), :]
                    got = more if got is None else got + more
                acc[half, y, t, rows, :] = got
            return carry

        lax.fori_loop(0, 8, place, 0)

    def rim_copies(half):
        return [
            pltpu.make_async_remote_copy(
                src_ref=rim.at[half, side],
                dst_ref=rims.at[half, side],
                send_sem=rim_send.at[half, side],
                recv_sem=rim_recv.at[half, side],
                device_id=(a, b, to_k),
                device_id_type=MESH,
            )
            for side, to_k in ((0, above), (1, below))
        ]

    def send_rims(half):
        for block in range(GX):
            rows = slice(8 * block, 8 * block + 8)
            up, low = zero, zero
            for y in range(8):
                turned = acc[half, y, 1, rows, :]
                turned = pltpu.roll(turned, 16 * y, 1) if y else turned
                up = jnp.where(lane // 16 == y, turned, up)
                low = jnp.where(lane // 16 == (y + 7) % 8, turned, low)
            rim[half, 0, rows, :] = up
            rim[half, 1, rows, :] = low
        for copy in rim_copies(half):
            copy.start()

    def whom(index):
        far = index // GY
        dz = 4 + ((far + 1) // 2) * (1 - 2 * lax.rem(far, 2))
        return wrap(a + dz, GX), wrap(b + lax.rem(index + 1, GY), GY)

    def part_copy(half, index):
        to_a, to_b = whom(index)
        return pltpu.make_async_remote_copy(
            src_ref=total.at[half, pl.ds(pl.multiple_of(16 * (GY * to_a + to_b), 16), 16)],
            dst_ref=parts.at[half, pl.ds(pl.multiple_of(16 * (GY * a + b), 16), 16)],
            send_sem=part_send.at[half, index],
            recv_sem=part_recv.at[half, index],
            device_id=(to_a, to_b, k),
            device_id_type=MESH,
        )

    def finish_owner(half, to_a, to_b, into, slot):
        rows = pl.ds(pl.multiple_of(8 * to_a, 8), 8)
        for h in range(2):
            y = 2 * to_b + h
            back = lax.rem(128 - 16 * y, 128)
            up = pltpu.roll(rims[half, 0, rows, :], back, 1)
            low = pltpu.roll(rims[half, 1, rows, :], back, 1)
            more = jnp.where(lane < 16, up, jnp.where(lane >= 112, low, 0.0))
            into[half, pl.ds(pl.multiple_of(16 * slot + 8 * h, 8), 8), :] = acc[half, y, 0, rows, :] + more

    def send_parts(half):
        for copy in rim_copies(half):
            copy.wait()

        def send_part(index, carry):
            to_a, to_b = whom(index)
            finish_owner(half, to_a, to_b, total, GY * to_a + to_b)

            @pl.when(index > 0)
            def _():
                part_copy(half, index - 1).start()

            return carry

        lax.fori_loop(0, OWNERS - 1, send_part, 0)
        finish_owner(half, a, b, parts, GY * a + b)
        part_copy(half, OWNERS - 2).start()

    def blend_group(half, step, first):
        weigh_group(half, step)
        for t in range(2):
            place_group(half, step, t, first)

    def blend_last(half, step):
        weigh_group(half, step)
        place_group(half, step, 1, False)
        send_rims(half)
        place_group(half, step, 0, False)

    blend_group(0, 0, True)
    blend_group(0, 1, False)
    blend_group(0, 3, False)
    blend_last(0, 2)
    blend_group(1, 0, True)
    send_parts(0)
    blend_group(1, 1, False)
    blend_group(1, 3, False)
    blend_last(1, 2)
    send_parts(1)

    for half in range(2):
        for step, turns in turns_of:
            for turn in turns:
                piece_copy(half, step, turn).wait_send()

        def await_part(index, carry, half=half):
            part_copy(half, index).wait()
            return carry

        lax.fori_loop(0, OWNERS - 1, await_part, 0)

    for x in range(BX):
        for h in range(2):
            for g in range(2):
                row = 8 * g * 16 + 8 * h + x
                norm = sums[4 * x + 2 * h + g]
                d1, d2 = [
                    (parts[half, pl.ds(row, 8, stride=16), :] + parts[half, pl.ds(row + 256, 8, stride=16), :]) / norm
                    for half in range(2)
                ]
                top = jnp.maximum(jnp.maximum(d1, d2), 0.0)
                e0, e1, e2 = jnp.exp(-top), jnp.exp(d1 - top), jnp.exp(d2 - top)
                scale = 1.0 / (e0 + e1 + e2)
                rows = slice(16 * h + 8 * g, 16 * h + 8 * g + 8)
                out_ref[x, 0, rows, :] = e0 * scale
                out_ref[x, 1, rows, :] = e1 * scale
                out_ref[x, 2, rows, :] = e2 * scale


def per_device(patch_logits, patch_start, patch_owner):
    tiles = patch_logits.reshape(GROUPS, 8, LAST + 1, 128)
    probs = pl.pallas_call(
        blend_kernel,
        out_shape=jax.ShapeDtypeStruct((BX, CLASSES, BY, BZ), F32),
        in_specs=[
            pl.BlockSpec(memory_space=pltpu.SMEM),
            pl.BlockSpec(memory_space=pltpu.SMEM),
            pl.BlockSpec(memory_space=pltpu.HBM),
        ],
        out_specs=pl.BlockSpec(memory_space=pltpu.VMEM),
        scratch_shapes=[
            pltpu.VMEM((GROUPS, LAST + 1, 8, 128), BF16),
            pltpu.VMEM((16, TILES[0], 8, 128), BF16),
            pltpu.VMEM((16, TILES[1], 8, 128), BF16),
            pltpu.VMEM((16, TILES[0], 8, 128), BF16),
            pltpu.VMEM((16, TILES[1], 8, 128), BF16),
            pltpu.VMEM((3 * PX, 8, 128), F32),
            pltpu.VMEM((32, 8, 128), F32),
            pltpu.VMEM((16, VROWS, 2, GROUPS, 8, 128), F32),
            pltpu.VMEM((4, VROWS + 1, 2, PX + 2 * MARGIN, 128), F32),
            pltpu.VMEM((2, 8, 2, 64, 128), F32),
            pltpu.VMEM((2, 2, 64, 128), F32),
            pltpu.VMEM((2, 2, 64, 128), F32),
            pltpu.VMEM((2, 16 * OWNERS, 128), F32),
            pltpu.VMEM((2, 16 * OWNERS, 128), F32),
            pltpu.SemaphoreType.DMA,
            pltpu.SemaphoreType.DMA((2, 16)),
            pltpu.SemaphoreType.DMA((2, 16)),
            pltpu.SemaphoreType.DMA((2, 2)),
            pltpu.SemaphoreType.DMA((2, 2)),
            pltpu.SemaphoreType.DMA((2, OWNERS)),
            pltpu.SemaphoreType.DMA((2, OWNERS)),
        ],
        compiler_params=pltpu.CompilerParams(collective_id=0, has_side_effects=True, vmem_limit_bytes=62000000),
    )(patch_owner, jnp.transpose(patch_start, (0, 3, 1, 2)), jnp.transpose(tiles, (0, 2, 1, 3)))
    return jnp.transpose(probs, (0, 2, 1, 3))


def solution(mesh):
    return jax.shard_map(
        per_device,
        mesh=mesh,
        in_specs=(P("gx", "gy", "gz", None, None), P(), P()),
        out_specs=P("gx", "gy", None, "gz"),
        check_vma=False,
    )
```

time: 52.7 us -> 54.2 us (1.028); the launches traced: 52.4 us -> 53.2 us
  Pallas kernels: 50.6 us -> 51.4 us
    pallas_call x1, Pallas kernels: 50.6 us -> 51.4 us  [per_device(): pl.pallas_call(blend_kernel, out_shape=jax.ShapeDtypeStruct((BX, CLASSES,...]
where the time goes in v3:
time: 54.2 us; the launch traced here: 53.2 us
  Pallas kernels  51.4 us (95%)
  local copies, waits for them, and re-layouts  1.77 us (3%)
    pallas_call x1, Pallas kernels, per_device(): pl.pallas_call(blend_kernel, out_shape=jax.ShapeDtypeStruct((BX, CLASSES,...  51.4 us
    unnamed x1, local copies, waits for them, and re-layouts  1.77 us

profile of v3, /device:TPU:1, one launch (start us, length us, event | category | flops | bytes accessed | tf_op | source)
XLA Modules:
  0.0 53.2 jit_solution(12360984127130602591)
XLA Ops:
  0.0 51.4 %shard_map.37 = f32[8,3,32,128]{3,2,1,0:T(8,128)} custom-call(s32[8,4,8]{2,1,0:T(4,128)} %owner_ref.1, s32[8,3,4,8]{3,2,1,0:T(4,128)} %bitcast.7, bf16[3,162,8,128]{3,2,1,0:T(8,128)(2,1)} %bitcast.6), custom_call_target="tpu_custom_call" | custom-call | tf_op jit(solution)/shard_map/pallas_call | solution.py:381
  51.5 1.8 %copy.5 = f32[8,32,3,128]{3,1,2,0:T(8,128)} copy(f32[8,32,3,128]{3,1,2,0:T(8,128)} %bitcast.5) | data formatting | bytes 786432

commit v4 on v3

--- a/solution.py
+++ b/solution.py
@@ -15,7 +15,8 @@
 GROUPS = PX // 8
 TILES = (21, 11)
 LAST = PY * ROW // 128 - 1
-MARGIN = 40
+MARGIN = 5
+SPAN = 13
 OWNERS = GX * GY
 F32 = jnp.float32
 BF16 = jnp.bfloat16
@@ -43,9 +44,9 @@
 
 
 def blend_kernel(
-    owner_ref, start_ref, x_ref, out_ref,
-    patch, send0, send1, recv0, recv1, table, sums, kept, value, acc, rim, rims, total, parts,
-    in_sem, send_sem, recv_sem, rim_send, rim_recv, part_send, part_recv,
+    owner_hbm, start_hbm, x_ref, out_ref,
+    owner_ref, start_ref, patch, send0, send1, recv0, recv1, table, sums, kept, value, acc, rim, rims, total, parts,
+    in_sem, owner_sem, start_sem, send_sem, recv_sem, rim_send, rim_recv, part_send, part_recv,
 ):
     a, b, k = lax.axis_index("gx"), lax.axis_index("gy"), lax.axis_index("gz")
     above, below = wrap(k + 1, GZ), wrap(k - 1, GZ)
@@ -58,6 +59,12 @@
         pl.semaphore_signal(barrier, inc=1, device_id=to, device_id_type=MESH)
     load = pltpu.make_async_copy(x_ref, patch, in_sem)
     load.start()
+    indices = [
+        pltpu.make_async_copy(owner_hbm, owner_ref, owner_sem),
+        pltpu.make_async_copy(start_hbm, start_ref, start_sem),
+    ]
+    for copy in indices:
+        copy.start()
 
     lane, sub = iota(1), iota(0)
     zero = jnp.zeros((8, 128), F32)
@@ -65,6 +72,8 @@
     def start_of(code, at_k, dim):
         return start_ref[code // GY, dim, lax.rem(code, GY), at_k]
 
+    for copy in indices:
+        copy.wait()
     my_sy = start_of(owner_ref[a, b, k], k, 1)
     load.wait()
 
@@ -149,11 +158,10 @@
 
     for s in range(4):
         for t in range(2):
-            for v in range(VROWS):
-                for row in (*range(0, MARGIN, 8), *range(MARGIN + PX, PX + 2 * MARGIN, 8)):
-                    value[s, v, t, row : row + 8, :] = zero
-            for row in range(0, PX + 2 * MARGIN, 8):
-                value[s, VROWS, t, row : row + 8, :] = zero
+            for v in range(VROWS + 1):
+                for at in range(SPAN):
+                    if v == VROWS or not MARGIN <= at < MARGIN + GROUPS + 1:
+                        value[s, v, t, at] = zero
     for offset in range(3 * PX):
         table[offset] = profile(jnp.full((8, 128), offset - PX, jnp.int32), PX)
 
@@ -205,10 +213,12 @@
 
             else:
                 piece_arrival(half, step, from_b).wait_recv()
-            _, _, rho, shift = corner(step, from_b)
+            sx, _, rho, shift = corner(step, from_b)
+            turn_x = lax.rem(sx, 8)
             along_z = [profile(c - shift, PZ) for c in columns]
             for v in range(VROWS):
                 along_y = profile(jnp.full((8, 128), RES * v, jnp.int32) + rho, PY)
+                turned = [[], []]
                 for g in range(GROUPS):
                     if half == 0:
                         pair = []
@@ -228,9 +238,13 @@
                         upper = aligned(first, second, shift, 16 * v)
                         base = [kept[slot, v, t, g] for t in range(2)]
                     along_xy = along_x[g] * along_y
-                    rows = slice(MARGIN + 8 * g, MARGIN + 8 * g + 8)
                     for t in range(2):
-                        value[from_b, v, t, rows, :] = (upper[t] - base[t]) * (along_xy * along_z[t])
+                        product = (upper[t] - base[t]) * (along_xy * along_z[t])
+                        turned[t].append(pltpu.roll(product, turn_x, 0))
+                for t in range(2):
+                    ends = [zero] + turned[t] + [zero]
+                    for g in range(GROUPS + 1):
+                        value[from_b, v, t, MARGIN + g] = jnp.where(sub < turn_x, ends[g], ends[g + 1])
             return carry
 
         lax.fori_loop(0, GY, weigh, 0)
@@ -242,12 +256,12 @@
             places = []
             for sx, first_y, _, _ in corners:
                 v = y - first_y
-                places.append((jnp.where((v >= 0) & (v < VROWS), v, VROWS), MARGIN - sx))
+                places.append((jnp.where((v >= 0) & (v < VROWS), v, VROWS), MARGIN - sx // 8))
             for block in range(GX):
                 rows = slice(8 * block, 8 * block + 8)
                 got = None if first else acc[half, y, t, rows, :]
-                for s, (v, row) in enumerate(places):
-                    more = value[s, v, t, pl.ds(row + 8 * block, 8), :]
+                for s, (v, at) in enumerate(places):
+                    more = value[s, v, t, at + block]
                     got = more if got is None else got + more
                 acc[half, y, t, rows, :] = got
             return carry
@@ -297,33 +311,39 @@
             device_id_type=MESH,
         )
 
-    def finish_owner(half, to_a, to_b, into, slot):
-        rows = pl.ds(pl.multiple_of(8 * to_a, 8), 8)
-        for h in range(2):
-            y = 2 * to_b + h
-            back = lax.rem(128 - 16 * y, 128)
-            up = pltpu.roll(rims[half, 0, rows, :], back, 1)
-            low = pltpu.roll(rims[half, 1, rows, :], back, 1)
-            more = jnp.where(lane < 16, up, jnp.where(lane >= 112, low, 0.0))
-            into[half, pl.ds(pl.multiple_of(16 * slot + 8 * h, 8), 8), :] = acc[half, y, 0, rows, :] + more
+    def finish_block(half, block, store):
+        rows = pl.ds(pl.multiple_of(8 * block, 8), 8)
+        up, low = rims[half, 0, rows, :], rims[half, 1, rows, :]
+        for y in range(8):
+            back = (128 - 16 * y) % 128
+            ends = (pltpu.roll(up, back, 1), pltpu.roll(low, back, 1)) if y else (up, low)
+            more = jnp.where(lane < 16, ends[0], jnp.where(lane >= 112, ends[1], 0.0))
+            store(y, acc[half, y, 0, rows, :] + more)
 
     def send_parts(half):
         for copy in rim_copies(half):
             copy.wait()
 
-        def send_part(index, carry):
-            to_a, to_b = whom(index)
-            finish_owner(half, to_a, to_b, total, GY * to_a + to_b)
-
-            @pl.when(index > 0)
+        def send_block(far, carry):
+            block, _ = whom(GY * far)
+
+            def store(y, what):
+                total[half, pl.ds(pl.multiple_of(64 * block + 8 * y, 8), 8), :] = what
+
+            finish_block(half, block, store)
+
+            @pl.when(far > 0)
             def _():
-                part_copy(half, index - 1).start()
+                for turn in range(GY):
+                    part_copy(half, GY * far - GY + turn).start()
 
             return carry
 
-        lax.fori_loop(0, OWNERS - 1, send_part, 0)
-        finish_owner(half, a, b, parts, GY * a + b)
-        part_copy(half, OWNERS - 2).start()
+        lax.fori_loop(0, GX, send_block, 0)
+        for turn in range(GY - 1):
+            part_copy(half, OWNERS - GY + turn).start()
+        mine = pl.ds(pl.multiple_of(16 * (GY * a + b), 16), 16)
+        parts[half, mine, :] = total[half, mine, :]
 
     def blend_group(half, step, first):
         weigh_group(half, step)
@@ -382,12 +402,14 @@
         blend_kernel,
         out_shape=jax.ShapeDtypeStruct((BX, CLASSES, BY, BZ), F32),
         in_specs=[
-            pl.BlockSpec(memory_space=pltpu.SMEM),
-            pl.BlockSpec(memory_space=pltpu.SMEM),
-            pl.BlockSpec(memory_space=pltpu.HBM),
+            pl.BlockSpec(memory_space=pl.ANY),
+            pl.BlockSpec(memory_space=pl.ANY),
+            pl.BlockSpec(memory_space=pl.ANY),
         ],
         out_specs=pl.BlockSpec(memory_space=pltpu.VMEM),
         scratch_shapes=[
+            pltpu.SMEM((GX, GY, GZ), jnp.int32),
+            pltpu.SMEM((GX, 3, GY, GZ), jnp.int32),
             pltpu.VMEM((GROUPS, LAST + 1, 8, 128), BF16),
             pltpu.VMEM((16, TILES[0], 8, 128), BF16),
             pltpu.VMEM((16, TILES[1], 8, 128), BF16),
@@ -396,12 +418,14 @@
             pltpu.VMEM((3 * PX, 8, 128), F32),
             pltpu.VMEM((32, 8, 128), F32),
             pltpu.VMEM((16, VROWS, 2, GROUPS, 8, 128), F32),
-            pltpu.VMEM((4, VROWS + 1, 2, PX + 2 * MARGIN, 128), F32),
+            pltpu.VMEM((4, VROWS + 1, 2, SPAN, 8, 128), F32),
             pltpu.VMEM((2, 8, 2, 64, 128), F32),
             pltpu.VMEM((2, 2, 64, 128), F32),
             pltpu.VMEM((2, 2, 64, 128), F32),
             pltpu.VMEM((2, 16 * OWNERS, 128), F32),
             pltpu.VMEM((2, 16 * OWNERS, 128), F32),
+            pltpu.SemaphoreType.DMA,
+            pltpu.SemaphoreType.DMA,
             pltpu.SemaphoreType.DMA,
             pltpu.SemaphoreType.DMA((2, 16)),
             pltpu.SemaphoreType.DMA((2, 16)),

time: 54.2 us -> 54.9 us (1.013); the launches traced: 53.2 us -> 54.7 us
  Pallas kernels: 51.4 us -> 52.9 us
    pallas_call x1, Pallas kernels: 51.4 us -> 52.9 us  [per_device(): pl.pallas_call(blend_kernel, out_shape=jax.ShapeDtypeStruct((BX, CLASSES,...]
where the time goes in v4:
time: 54.9 us; the launch traced here: 54.7 us
  Pallas kernels  52.9 us (96%)
  local copies, waits for them, and re-layouts  1.77 us (3%)
    pallas_call x1, Pallas kernels, per_device(): pl.pallas_call(blend_kernel, out_shape=jax.ShapeDtypeStruct((BX, CLASSES,...  52.9 us
    unnamed x1, local copies, waits for them, and re-layouts  1.77 us

profile of v4, /device:TPU:1, one launch (start us, length us, event | category | flops | bytes accessed | tf_op | source)
XLA Modules:
  0.0 54.7 jit_solution(126152411100982934)
XLA Ops:
  0.0 52.9 %shard_map.37 = f32[8,3,32,128]{3,2,1,0:T(8,128)} custom-call(s32[8,4,8]{2,1,0:T(4,128)} %owner_hbm.1, s32[8,3,4,8]{3,2,1,0:T(4,128)} %bitcast.7, bf16[3,162,8,128]{3,2,1,0:T(8,128)(2,1)} %bitcast.6), custom_call_target="tpu_custom_call" | custom-call | tf_op jit(solution)/shard_map/pallas_call | solution.py:401
  52.9 1.8 %copy.5 = f32[8,32,3,128]{3,1,2,0:T(8,128)} copy(f32[8,32,3,128]{3,1,2,0:T(8,128)} %bitcast.5) | data formatting | bytes 786432

commit v5 on v4

--- a/solution.py
+++ b/solution.py
@@ -218,7 +218,7 @@
             along_z = [profile(c - shift, PZ) for c in columns]
             for v in range(VROWS):
                 along_y = profile(jnp.full((8, 128), RES * v, jnp.int32) + rho, PY)
-                turned = [[], []]
+                turned, bases = [[], []], []
                 for g in range(GROUPS):
                     if half == 0:
                         pair = []
@@ -226,8 +226,7 @@
                             ends = recv0[slot, GROUPS * m + g], recv0[slot, GROUPS * m + GROUPS + g]
                             pair.append(aligned(*ends, shift, 16 * m))
                         base, upper = pair
-                        for t in range(2):
-                            kept[slot, v, t, g] = base[t]
+                        bases.append(base)
                     else:
                         first = recv1[slot, GROUPS * v + g].astype(F32)
                         if v < VROWS - 1:
@@ -241,6 +240,9 @@
                     for t in range(2):
                         product = (upper[t] - base[t]) * (along_xy * along_z[t])
                         turned[t].append(pltpu.roll(product, turn_x, 0))
+                for g, base in enumerate(bases):
+                    for t in range(2):
+                        kept[slot, v, t, g] = base[t]
                 for t in range(2):
                     ends = [zero] + turned[t] + [zero]
                     for g in range(GROUPS + 1):
@@ -249,7 +251,7 @@
 
         lax.fori_loop(0, GY, weigh, 0)
 
-    def place_group(half, step, t, first):
+    def place_group(half, step, lane_tiles, first):
         corners = [corner(step, from_b) for from_b in range(GY)]
 
         def place(y, carry):
@@ -257,13 +259,16 @@
             for sx, first_y, _, _ in corners:
                 v = y - first_y
                 places.append((jnp.where((v >= 0) & (v < VROWS), v, VROWS), MARGIN - sx // 8))
-            for block in range(GX):
-                rows = slice(8 * block, 8 * block + 8)
-                got = None if first else acc[half, y, t, rows, :]
-                for s, (v, at) in enumerate(places):
-                    more = value[s, v, t, at + block]
-                    got = more if got is None else got + more
-                acc[half, y, t, rows, :] = got
+            sums_of = {}
+            for t in lane_tiles:
+                for block in range(GX):
+                    one, two, three, four = [value[s, v, t, at + block] for s, (v, at) in enumerate(places)]
+                    got = (one + two) + (three + four)
+                    if not first:
+                        got = got + acc[half, y, t, 8 * block : 8 * block + 8, :]
+                    sums_of[t, block] = got
+            for (t, block), got in sums_of.items():
+                acc[half, y, t, 8 * block : 8 * block + 8, :] = got
             return carry
 
         lax.fori_loop(0, 8, place, 0)
@@ -311,14 +316,17 @@
             device_id_type=MESH,
         )
 
-    def finish_block(half, block, store):
+    def finish_block(half, block):
         rows = pl.ds(pl.multiple_of(8 * block, 8), 8)
         up, low = rims[half, 0, rows, :], rims[half, 1, rows, :]
+        cells = []
         for y in range(8):
             back = (128 - 16 * y) % 128
             ends = (pltpu.roll(up, back, 1), pltpu.roll(low, back, 1)) if y else (up, low)
             more = jnp.where(lane < 16, ends[0], jnp.where(lane >= 112, ends[1], 0.0))
-            store(y, acc[half, y, 0, rows, :] + more)
+            cells.append(acc[half, y, 0, rows, :] + more)
+        for y, what in enumerate(cells):
+            total[half, pl.ds(pl.multiple_of(64 * block + 8 * y, 8), 8), :] = what
 
     def send_parts(half):
         for copy in rim_copies(half):
@@ -326,11 +334,7 @@
 
         def send_block(far, carry):
             block, _ = whom(GY * far)
-
-            def store(y, what):
-                total[half, pl.ds(pl.multiple_of(64 * block + 8 * y, 8), 8), :] = what
-
-            finish_block(half, block, store)
+            finish_block(half, block)
 
             @pl.when(far > 0)
             def _():
@@ -347,14 +351,13 @@
 
     def blend_group(half, step, first):
         weigh_group(half, step)
-        for t in range(2):
-            place_group(half, step, t, first)
+        place_group(half, step, (0, 1), first)
 
     def blend_last(half, step):
         weigh_group(half, step)
-        place_group(half, step, 1, False)
+        place_group(half, step, (1,), False)
         send_rims(half)
-        place_group(half, step, 0, False)
+        place_group(half, step, (0,), False)
 
     blend_group(0, 0, True)
     blend_group(0, 1, False)

time: 54.9 us -> 51.1 us (0.931)
  Pallas kernels: 52.9 us -> 49.2 us
    pallas_call x1, Pallas kernels: 52.9 us -> 49.2 us  [per_device(): pl.pallas_call(blend_kernel, out_shape=jax.ShapeDtypeStruct((BX, CLASSES,...]
where the time goes in v5:
time: 51.1 us; the launch traced here: 50.9 us
  Pallas kernels  49.2 us (96%)
  local copies, waits for them, and re-layouts  1.77 us (3%)
    pallas_call x1, Pallas kernels, per_device(): pl.pallas_call(blend_kernel, out_shape=jax.ShapeDtypeStruct((BX, CLASSES,...  49.2 us
    unnamed x1, local copies, waits for them, and re-layouts  1.77 us

profile of v5, /device:TPU:1, one launch (start us, length us, event | category | flops | bytes accessed | tf_op | source)
XLA Modules:
  0.0 50.9 jit_solution(12689420239871885581)
XLA Ops:
  0.0 49.2 %shard_map.37 = f32[8,3,32,128]{3,2,1,0:T(8,128)} custom-call(s32[8,4,8]{2,1,0:T(4,128)} %owner_hbm.1, s32[8,3,4,8]{3,2,1,0:T(4,128)} %bitcast.7, bf16[3,162,8,128]{3,2,1,0:T(8,128)(2,1)} %bitcast.6), custom_call_target="tpu_custom_call" | custom-call | tf_op jit(solution)/shard_map/pallas_call | solution.py:404
  49.2 1.8 %copy.5 = f32[8,32,3,128]{3,1,2,0:T(8,128)} copy(f32[8,32,3,128]{3,1,2,0:T(8,128)} %bitcast.5) | data formatting | bytes 786432

commit v6 on v5

--- a/solution.py
+++ b/solution.py
@@ -36,11 +36,15 @@
 
 
 def wrap(index, size):
-    return lax.rem(index + size, size)
+    return index & (size - 1)
+
+
+def halved(index, times):
+    return lax.shift_right_logical(index, jnp.int32(times))
 
 
 def hop_of(step, to_b):
-    return (0, 1, 2 - 4 * lax.rem(to_b, 2), -1)[step]
+    return (0, 1, 2 - 4 * (to_b & 1), -1)[step]
 
 
 def blend_kernel(
@@ -70,7 +74,7 @@
     zero = jnp.zeros((8, 128), F32)
 
     def start_of(code, at_k, dim):
-        return start_ref[code // GY, dim, lax.rem(code, GY), at_k]
+        return start_ref[halved(code, 2), dim, code & (GY - 1), at_k]
 
     for copy in indices:
         copy.wait()
@@ -78,14 +82,16 @@
     load.wait()
 
     def cut(residue, store):
-        rho = lax.rem(residue - my_sy + 8 * RES, RES)
-        for half, (skip, length) in enumerate(((0, 2 * PZ), (2 * PZ, PZ))):
-            for g in range(GROUPS):
+        rho = (residue - my_sy) & (RES - 1)
+        tails = []
+        for g in range(GROUPS):
+            done = []
+            for half, (skip, length) in enumerate(((0, 2 * PZ), (2 * PZ, PZ))):
                 tiles = {}
                 for v in range(VROWS):
                     into = length * v
                     delta = ROW * rho + (ROW * RES * v + skip - into)
-                    first = (delta + 127) // 128
+                    first = halved(delta + 127, 7)
                     turn = first * 128 - delta
                     low, high = into // 128, (into + length - 1) // 128
                     turned = []
@@ -99,15 +105,14 @@
                     for t in range(low, high + 1):
                         tile = jnp.where(lane < turn, turned[t - low], turned[t - low + 1])
                         tiles[t] = jnp.where(lane < into % 128, tiles[t], tile) if t in tiles else tile
-                for t in range(7 if half == 0 else 3):
-                    store(half, GROUPS * t + g, tiles[t].astype(BF16))
-                if half == 1:
-                    if g == 0:
-                        tail = tiles[3]
-                    elif g == 1:
-                        store(1, 9, jnp.where(lane < 48, tail, pltpu.roll(tiles[3], 48, 1)).astype(BF16))
-                    else:
-                        store(1, 10, tiles[3].astype(BF16))
+                done.append(tiles)
+            for t in range(7):
+                store(0, GROUPS * t + g, done[0][t].astype(BF16))
+            for t in range(3):
+                store(1, GROUPS * t + g, done[1][t].astype(BF16))
+            tails.append(done[1][3])
+        store(1, 9, jnp.where(lane < 48, tails[0], pltpu.roll(tails[1], 48, 1)).astype(BF16))
+        store(1, 10, tails[2].astype(BF16))
 
     def piece_copy(half, step, turn):
         to_b = wrap(b + turn, GY)
@@ -134,7 +139,7 @@
     for step, turns in turns_of:
 
         def cut_one(turn, carry, step=step):
-            residue = 4 * lax.rem(a + step, 4) + wrap(b + turn, GY)
+            residue = 4 * wrap(a + step, 4) + wrap(b + turn, GY)
 
             def store(half, tile, what):
                 send[half][4 * step + turn, tile] = what
@@ -154,7 +159,7 @@
     def store_own(half, tile, what):
         recv[half][b, tile] = what
 
-    cut(4 * lax.rem(a, 4) + b, store_own)
+    cut(4 * wrap(a, 4) + b, store_own)
 
     for s in range(4):
         for t in range(2):
@@ -166,7 +171,7 @@
         table[offset] = profile(jnp.full((8, 128), offset - PX, jnp.int32), PX)
 
     def add_weight(index, carry):
-        i, j, at_k = a - 2 + index // 9, b - 1 + lax.rem(index // 3, 3), k - 1 + lax.rem(index, 3)
+        i, j, at_k = a - 2 + lax.div(index, 9), b - 1 + lax.rem(lax.div(index, 3), 3), k - 1 + lax.rem(index, 3)
         valid = (i >= 0) & (i < GX) & (j >= 0) & (j < GY) & (at_k >= 0) & (at_k < GZ)
         i, j, at_k = jnp.clip(i, 0, GX - 1), jnp.clip(j, 0, GY - 1), jnp.clip(at_k, 0, GZ - 1)
         along_z = profile(BZ * k + lane - start_ref[i, 2, j, at_k], PZ)
@@ -184,7 +189,7 @@
     for at in range(32):
         sums[at] = weights[at]
 
-    residue = 4 * lax.rem(a, 4) + b
+    residue = 4 * wrap(a, 4) + b
     along_x = [profile(sub + 8 * g, PX) for g in range(GROUPS)]
     columns = (lane, jnp.where(lane < 64, lane + 128, lane - 128))
 
@@ -192,13 +197,13 @@
         from_a = wrap(a - hop_of(step, b), GX)
         code = owner_ref[from_a, from_b, k]
         sy = start_of(code, k, 1)
-        rho = lax.rem(residue - sy + 8 * RES, RES)
-        return start_of(code, k, 0), (sy + rho) // RES, rho, start_of(code, k, 2) - BZ * k
+        rho = (residue - sy) & (RES - 1)
+        return start_of(code, k, 0), halved(sy + rho, 4), rho, start_of(code, k, 2) - BZ * k
 
     def aligned(first, second, shift, lead):
-        turn = lax.rem(shift - lead + 512, 256)
-        low = lax.rem(turn, 128)
-        swap = (jnp.where(lane < low, 1, 0) + turn // 128) == 1
+        turn = (shift - lead) & 255
+        low = turn & 127
+        swap = (jnp.where(lane < low, 1, 0) + halved(turn, 7)) == 1
         first, second = pltpu.roll(first.astype(F32), low, 1), pltpu.roll(second.astype(F32), low, 1)
         return jnp.where(swap, second, first), jnp.where(swap, first, second)
 
@@ -214,35 +219,36 @@
             else:
                 piece_arrival(half, step, from_b).wait_recv()
             sx, _, rho, shift = corner(step, from_b)
-            turn_x = lax.rem(sx, 8)
+            turn_x = sx & 7
             along_z = [profile(c - shift, PZ) for c in columns]
+            held = {}
+            for v in range(VROWS):
+                for g in range(GROUPS):
+                    if half == 0:
+                        for m in (2 * v, 2 * v + 1):
+                            held[m, g] = recv0[slot, GROUPS * m + g], recv0[slot, GROUPS * m + GROUPS + g]
+                    else:
+                        tail = 9 + g // 2 if v == VROWS - 1 else GROUPS * v + GROUPS + g
+                        held[v, g] = recv1[slot, GROUPS * v + g], recv1[slot, tail]
+                        held[v, g, 0] = [kept[slot, v, t, g] for t in range(2)]
             for v in range(VROWS):
                 along_y = profile(jnp.full((8, 128), RES * v, jnp.int32) + rho, PY)
-                turned, bases = [[], []], []
+                turned = [[], []]
                 for g in range(GROUPS):
                     if half == 0:
-                        pair = []
-                        for m in (2 * v, 2 * v + 1):
-                            ends = recv0[slot, GROUPS * m + g], recv0[slot, GROUPS * m + GROUPS + g]
-                            pair.append(aligned(*ends, shift, 16 * m))
-                        base, upper = pair
-                        bases.append(base)
+                        base, upper = [aligned(*held[m, g], shift, 16 * m) for m in (2 * v, 2 * v + 1)]
+                        for t in range(2):
+                            kept[slot, v, t, g] = base[t]
                     else:
-                        first = recv1[slot, GROUPS * v + g].astype(F32)
-                        if v < VROWS - 1:
-                            second = recv1[slot, GROUPS * v + GROUPS + g].astype(F32)
-                        else:
-                            second = recv1[slot, 9 + g // 2].astype(F32)
-                            second = pltpu.roll(second, 80, 1) if g == 1 else second
+                        first, second = held[v, g]
+                        if v == VROWS - 1 and g == 1:
+                            second = pltpu.roll(second.astype(F32), 80, 1)
                         upper = aligned(first, second, shift, 16 * v)
-                        base = [kept[slot, v, t, g] for t in range(2)]
+                        base = held[v, g, 0]
                     along_xy = along_x[g] * along_y
                     for t in range(2):
                         product = (upper[t] - base[t]) * (along_xy * along_z[t])
                         turned[t].append(pltpu.roll(product, turn_x, 0))
-                for g, base in enumerate(bases):
-                    for t in range(2):
-                        kept[slot, v, t, g] = base[t]
                 for t in range(2):
                     ends = [zero] + turned[t] + [zero]
                     for g in range(GROUPS + 1):
@@ -258,11 +264,12 @@
             places = []
             for sx, first_y, _, _ in corners:
                 v = y - first_y
-                places.append((jnp.where((v >= 0) & (v < VROWS), v, VROWS), MARGIN - sx // 8))
+                places.append((jnp.where((v >= 0) & (v < VROWS), v, VROWS), MARGIN - halved(sx, 3)))
+            loaded = [{t: value[s, v, t, pl.ds(at, GX)] for t in lane_tiles} for s, (v, at) in enumerate(places)]
             sums_of = {}
             for t in lane_tiles:
                 for block in range(GX):
-                    one, two, three, four = [value[s, v, t, at + block] for s, (v, at) in enumerate(places)]
+                    one, two, three, four = [tiles[t][block] for tiles in loaded]
                     got = (one + two) + (three + four)
                     if not first:
                         got = got + acc[half, y, t, 8 * block : 8 * block + 8, :]
@@ -301,9 +308,9 @@
             copy.start()
 
     def whom(index):
-        far = index // GY
-        dz = 4 + ((far + 1) // 2) * (1 - 2 * lax.rem(far, 2))
-        return wrap(a + dz, GX), wrap(b + lax.rem(index + 1, GY), GY)
+        far = halved(index, 2)
+        dz = 4 + halved(far + 1, 1) * (1 - 2 * (far & 1))
+        return wrap(a + dz, GX), wrap(b + index + 1, GY)
 
     def part_copy(half, index):
         to_a, to_b = whom(index)
@@ -333,7 +340,7 @@
             copy.wait()
 
         def send_block(far, carry):
-            block, _ = whom(GY * far)
+            block, _ = whom(jnp.int32(GY) * far)
             finish_block(half, block)
 
             @pl.when(far > 0)

time: 51.1 us -> 47.8 us (0.935)
  Pallas kernels: 49.2 us -> 45.8 us
    pallas_call x1, Pallas kernels: 49.2 us -> 45.8 us  [per_device(): pl.pallas_call(blend_kernel, out_shape=jax.ShapeDtypeStruct((BX, CLASSES,...]
where the time goes in v6:
time: 47.8 us; the launch traced here: 47.6 us
  Pallas kernels  45.8 us (96%)
  local copies, waits for them, and re-layouts  1.77 us (4%)
    pallas_call x1, Pallas kernels, per_device(): pl.pallas_call(blend_kernel, out_shape=jax.ShapeDtypeStruct((BX, CLASSES,...  45.8 us
    unnamed x1, local copies, waits for them, and re-layouts  1.77 us

profile of v6, /device:TPU:1, one launch (start us, length us, event | category | flops | bytes accessed | tf_op | source)
XLA Modules:
  0.0 47.6 jit_solution(9609065936334119887)
XLA Ops:
  0.0 45.8 %shard_map.37 = f32[8,3,32,128]{3,2,1,0:T(8,128)} custom-call(s32[8,4,8]{2,1,0:T(4,128)} %owner_hbm.1, s32[8,3,4,8]{3,2,1,0:T(4,128)} %bitcast.7, bf16[3,162,8,128]{3,2,1,0:T(8,128)(2,1)} %bitcast.6), custom_call_target="tpu_custom_call" | custom-call | tf_op jit(solution)/shard_map/pallas_call | solution.py:411
  45.8 1.8 %copy.5 = f32[8,32,3,128]{3,1,2,0:T(8,128)} copy(f32[8,32,3,128]{3,1,2,0:T(8,128)} %bitcast.5) | data formatting | bytes 786432

commit v7 on v6

--- a/solution.py
+++ b/solution.py
@@ -21,6 +21,7 @@
 F32 = jnp.float32
 BF16 = jnp.bfloat16
 MESH = pl.DeviceIdType.MESH
+ORDER = (2, 1, 3, 0)
 
 
 def profile(offsets, length):
@@ -135,7 +136,7 @@
             device_id_type=MESH,
         )
 
-    turns_of = ((2, range(GY)), (1, range(GY)), (3, range(GY)), (0, range(1, GY)))
+    turns_of = [(step, [turn for turn in ORDER if step or turn]) for step in ORDER]
     for step, turns in turns_of:
 
         def cut_one(turn, carry, step=step):
@@ -147,7 +148,7 @@
             cut(residue, store)
             return carry
 
-        lax.fori_loop(turns.start, GY, cut_one, 0)
+        lax.fori_loop(GY - len(turns), GY, cut_one, 0)
         if step == 2:
             pl.semaphore_wait(barrier, len(near))
         for turn in turns:
@@ -307,18 +308,16 @@
         for copy in rim_copies(half):
             copy.start()
 
-    def whom(index):
-        far = halved(index, 2)
-        dz = 4 + halved(far + 1, 1) * (1 - 2 * (far & 1))
-        return wrap(a + dz, GX), wrap(b + index + 1, GY)
-
-    def part_copy(half, index):
-        to_a, to_b = whom(index)
+    def block_of(far):
+        return wrap(a + 4 + halved(far + 1, 1) * (1 - 2 * (far & 1)), GX)
+
+    def part_copy(half, far, turn):
+        to_a, to_b = block_of(far), wrap(b + ORDER[turn], GY)
         return pltpu.make_async_remote_copy(
             src_ref=total.at[half, pl.ds(pl.multiple_of(16 * (GY * to_a + to_b), 16), 16)],
             dst_ref=parts.at[half, pl.ds(pl.multiple_of(16 * (GY * a + b), 16), 16)],
-            send_sem=part_send.at[half, index],
-            recv_sem=part_recv.at[half, index],
+            send_sem=part_send.at[half, GY * far + turn],
+            recv_sem=part_recv.at[half, GY * far + turn],
             device_id=(to_a, to_b, k),
             device_id_type=MESH,
         )
@@ -340,19 +339,18 @@
             copy.wait()
 
         def send_block(far, carry):
-            block, _ = whom(jnp.int32(GY) * far)
-            finish_block(half, block)
+            finish_block(half, block_of(far))
 
             @pl.when(far > 0)
             def _():
                 for turn in range(GY):
-                    part_copy(half, GY * far - GY + turn).start()
+                    part_copy(half, far - 1, turn).start()
 
             return carry
 
         lax.fori_loop(0, GX, send_block, 0)
         for turn in range(GY - 1):
-            part_copy(half, OWNERS - GY + turn).start()
+            part_copy(half, jnp.int32(GX - 1), turn).start()
         mine = pl.ds(pl.multiple_of(16 * (GY * a + b), 16), 16)
         parts[half, mine, :] = total[half, mine, :]
 
@@ -382,11 +380,17 @@
             for turn in turns:
                 piece_copy(half, step, turn).wait_send()
 
-        def await_part(index, carry, half=half):
-            part_copy(half, index).wait()
+        def await_parts(far, carry, half=half):
+            for turn in range(GY - 1):
+                part_copy(half, far, turn).wait()
+
+            @pl.when(far < GX - 1)
+            def _():
+                part_copy(half, far, GY - 1).wait()
+
             return carry
 
-        lax.fori_loop(0, OWNERS - 1, await_part, 0)
+        lax.fori_loop(0, GX, await_parts, 0)
 
     for x in range(BX):
         for h in range(2):

time: 47.8 us -> 47.4 us (level)
  Pallas kernels: 45.8 us -> 45.2 us
    pallas_call x1, Pallas kernels: 45.8 us -> 45.2 us  [per_device(): pl.pallas_call(blend_kernel, out_shape=jax.ShapeDtypeStruct((BX, CLASSES,...]
where the time goes in v7:
time: 47.4 us; the launch traced here: 46.9 us
  Pallas kernels  45.2 us (95%)
  local copies, waits for them, and re-layouts  1.77 us (4%)
    pallas_call x1, Pallas kernels, per_device(): pl.pallas_call(blend_kernel, out_shape=jax.ShapeDtypeStruct((BX, CLASSES,...  45.2 us
    unnamed x1, local copies, waits for them, and re-layouts  1.77 us

profile of v7, /device:TPU:1, one launch (start us, length us, event | category | flops | bytes accessed | tf_op | source)
XLA Modules:
  0.0 46.9 jit_solution(8466064574719609440)
XLA Ops:
  0.0 45.2 %shard_map.37 = f32[8,3,32,128]{3,2,1,0:T(8,128)} custom-call(s32[8,4,8]{2,1,0:T(4,128)} %owner_hbm.1, s32[8,3,4,8]{3,2,1,0:T(4,128)} %bitcast.7, bf16[3,162,8,128]{3,2,1,0:T(8,128)(2,1)} %bitcast.6), custom_call_target="tpu_custom_call" | custom-call | tf_op jit(solution)/shard_map/pallas_call | solution.py:415
  45.2 1.8 %copy.5 = f32[8,32,3,128]{3,1,2,0:T(8,128)} copy(f32[8,32,3,128]{3,1,2,0:T(8,128)} %bitcast.5) | data formatting | bytes 786432

commit v8 on v7

--- a/solution.py
+++ b/solution.py
@@ -153,10 +153,6 @@
             pl.semaphore_wait(barrier, len(near))
         for turn in turns:
             piece_copy(0, step, turn).start()
-    for step, turns in turns_of:
-        for turn in turns:
-            piece_copy(1, step, turn).start()
-
     def store_own(half, tile, what):
         recv[half][b, tile] = what
 
@@ -364,21 +360,30 @@
         send_rims(half)
         place_group(half, step, (0,), False)
 
-    blend_group(0, 0, True)
+    def send_rest(*steps):
+        for step, turns in turns_of:
+            for turn in turns if step in steps else ():
+                piece_copy(0, step, turn).wait_send()
+                piece_copy(1, step, turn).start()
+
+    blend_group(0, 2, True)
+    send_rest(2)
     blend_group(0, 1, False)
+    send_rest(1)
     blend_group(0, 3, False)
-    blend_last(0, 2)
-    blend_group(1, 0, True)
+    send_rest(3, 0)
+    blend_last(0, 0)
+    blend_group(1, 2, True)
     send_parts(0)
     blend_group(1, 1, False)
     blend_group(1, 3, False)
-    blend_last(1, 2)
+    blend_last(1, 0)
     send_parts(1)
 
+    for step, turns in turns_of:
+        for turn in turns:
+            piece_copy(1, step, turn).wait_send()
     for half in range(2):
-        for step, turns in turns_of:
-            for turn in turns:
-                piece_copy(half, step, turn).wait_send()
 
         def await_parts(far, carry, half=half):
             for turn in range(GY - 1):

time: 47.4 us -> 44.5 us (0.939)
  Pallas kernels: 45.2 us -> 42.6 us
    pallas_call x1, Pallas kernels: 45.2 us -> 42.6 us  [per_device(): pl.pallas_call(blend_kernel, out_shape=jax.ShapeDtypeStruct((BX, CLASSES,...]
where the time goes in v8:
time: 44.5 us; the launch traced here: 44.4 us
  Pallas kernels  42.6 us (96%)
  local copies, waits for them, and re-layouts  1.77 us (4%)
    pallas_call x1, Pallas kernels, per_device(): pl.pallas_call(blend_kernel, out_shape=jax.ShapeDtypeStruct((BX, CLASSES,...  42.6 us
    unnamed x1, local copies, waits for them, and re-layouts  1.77 us

profile of v8, /device:TPU:1, one launch (start us, length us, event | category | flops | bytes accessed | tf_op | source)
XLA Modules:
  0.0 44.4 jit_solution(11064289752397070882)
XLA Ops:
  0.0 42.6 %shard_map.37 = f32[8,3,32,128]{3,2,1,0:T(8,128)} custom-call(s32[8,4,8]{2,1,0:T(4,128)} %owner_hbm.1, s32[8,3,4,8]{3,2,1,0:T(4,128)} %bitcast.7, bf16[3,162,8,128]{3,2,1,0:T(8,128)(2,1)} %bitcast.6), custom_call_target="tpu_custom_call" | custom-call | tf_op jit(solution)/shard_map/pallas_call | solution.py:420
  42.6 1.8 %copy.5 = f32[8,32,3,128]{3,1,2,0:T(8,128)} copy(f32[8,32,3,128]{3,1,2,0:T(8,128)} %bitcast.5) | data formatting | bytes 786432

commit v9 on v8

--- a/solution.py
+++ b/solution.py
@@ -12,6 +12,7 @@
 ROW = CLASSES * PZ
 RES = 16
 VROWS = PY // RES
+SLOTS = 16
 GROUPS = PX // 8
 TILES = (21, 11)
 LAST = PY * ROW // 128 - 1
@@ -82,38 +83,36 @@
     my_sy = start_of(owner_ref[a, b, k], k, 1)
     load.wait()
 
-    def cut(residue, store):
+    def cut(half, residue, store):
         rho = (residue - my_sy) & (RES - 1)
+        skip, length = ((0, 2 * PZ), (2 * PZ, PZ))[half]
         tails = []
         for g in range(GROUPS):
-            done = []
-            for half, (skip, length) in enumerate(((0, 2 * PZ), (2 * PZ, PZ))):
-                tiles = {}
-                for v in range(VROWS):
-                    into = length * v
-                    delta = ROW * rho + (ROW * RES * v + skip - into)
-                    first = halved(delta + 127, 7)
-                    turn = first * 128 - delta
-                    low, high = into // 128, (into + length - 1) // 128
-                    turned = []
-                    for t in range(low - 1, high + 1):
-                        at = first + t
-                        if t < 0:
-                            at = jnp.maximum(at, 0)
-                        if half == 1 and v == VROWS - 1 and t == high:
-                            at = jnp.minimum(at, LAST)
-                        turned.append(pltpu.roll(patch[g, at].astype(F32), turn, 1))
-                    for t in range(low, high + 1):
-                        tile = jnp.where(lane < turn, turned[t - low], turned[t - low + 1])
-                        tiles[t] = jnp.where(lane < into % 128, tiles[t], tile) if t in tiles else tile
-                done.append(tiles)
-            for t in range(7):
-                store(0, GROUPS * t + g, done[0][t].astype(BF16))
-            for t in range(3):
-                store(1, GROUPS * t + g, done[1][t].astype(BF16))
-            tails.append(done[1][3])
-        store(1, 9, jnp.where(lane < 48, tails[0], pltpu.roll(tails[1], 48, 1)).astype(BF16))
-        store(1, 10, tails[2].astype(BF16))
+            tiles = {}
+            for v in range(VROWS):
+                into = length * v
+                delta = ROW * rho + (ROW * RES * v + skip - into)
+                first = halved(delta + 127, 7)
+                turn = first * 128 - delta
+                low, high = into // 128, (into + length - 1) // 128
+                turned = []
+                for t in range(low - 1, high + 1):
+                    at = first + t
+                    if t < 0:
+                        at = jnp.maximum(at, 0)
+                    if half == 1 and v == VROWS - 1 and t == high:
+                        at = jnp.minimum(at, LAST)
+                    turned.append(pltpu.roll(patch[g, at].astype(F32), turn, 1))
+                for t in range(low, high + 1):
+                    tile = jnp.where(lane < turn, turned[t - low], turned[t - low + 1])
+                    tiles[t] = jnp.where(lane < into % 128, tiles[t], tile) if t in tiles else tile
+            for t in range(7 if half == 0 else 3):
+                store(GROUPS * t + g, tiles[t].astype(BF16))
+            if half == 1:
+                tails.append(tiles[3])
+        if half == 1:
+            store(9, jnp.where(lane < 48, tails[0], pltpu.roll(tails[1], 48, 1)).astype(BF16))
+            store(10, tails[2].astype(BF16))
 
     def piece_copy(half, step, turn):
         to_b = wrap(b + turn, GY)
@@ -137,54 +136,44 @@
         )
 
     turns_of = [(step, [turn for turn in ORDER if step or turn]) for step in ORDER]
+    def cut_step(half, step):
+        def cut_one(turn, carry):
+            def store(tile, what):
+                send[half][4 * step + turn, tile] = what
+
+            cut(half, 4 * wrap(a + step, 4) + wrap(b + turn, GY), store)
+            return carry
+
+        lax.fori_loop(0 if step else 1, GY, cut_one, 0)
+
+    def cut_own(half):
+        def store(tile, what):
+            recv[half][b, tile] = what
+
+        cut(half, 4 * wrap(a, 4) + b, store)
+
     for step, turns in turns_of:
-
-        def cut_one(turn, carry, step=step):
-            residue = 4 * wrap(a + step, 4) + wrap(b + turn, GY)
-
-            def store(half, tile, what):
-                send[half][4 * step + turn, tile] = what
-
-            cut(residue, store)
-            return carry
-
-        lax.fori_loop(GY - len(turns), GY, cut_one, 0)
+        cut_step(0, step)
         if step == 2:
             pl.semaphore_wait(barrier, len(near))
         for turn in turns:
             piece_copy(0, step, turn).start()
-    def store_own(half, tile, what):
-        recv[half][b, tile] = what
-
-    cut(4 * wrap(a, 4) + b, store_own)
-
-    for s in range(4):
+    cut_own(0)
+    for step, _ in turns_of:
+        cut_step(1, step)
+    cut_own(1)
+
+    for t in range(2):
+        for at in range(SPAN):
+            value[SLOTS * VROWS, t, at] = zero
+
+    def clear(at, carry):
         for t in range(2):
-            for v in range(VROWS + 1):
-                for at in range(SPAN):
-                    if v == VROWS or not MARGIN <= at < MARGIN + GROUPS + 1:
-                        value[s, v, t, at] = zero
-    for offset in range(3 * PX):
-        table[offset] = profile(jnp.full((8, 128), offset - PX, jnp.int32), PX)
-
-    def add_weight(index, carry):
-        i, j, at_k = a - 2 + lax.div(index, 9), b - 1 + lax.rem(lax.div(index, 3), 3), k - 1 + lax.rem(index, 3)
-        valid = (i >= 0) & (i < GX) & (j >= 0) & (j < GY) & (at_k >= 0) & (at_k < GZ)
-        i, j, at_k = jnp.clip(i, 0, GX - 1), jnp.clip(j, 0, GY - 1), jnp.clip(at_k, 0, GZ - 1)
-        along_z = profile(BZ * k + lane - start_ref[i, 2, j, at_k], PZ)
-        along_z = along_z * jnp.where(valid, 1.0, 0.0)
-        y = BY * b + sub - start_ref[i, 1, j, at_k]
-        planes = [profile(y + 8 * g, PY) * along_z for g in range(4)]
-        base = jnp.clip(BX * a - start_ref[i, 0, j, at_k] + PX, 0, 2 * PX)
-        new = []
-        for x in range(BX):
-            along_x = table[base + x]
-            new += [carry[4 * x + g] + along_x * planes[g] for g in range(4)]
-        return tuple(new)
-
-    weights = lax.fori_loop(0, 45, add_weight, (zero,) * 32)
-    for at in range(32):
-        sums[at] = weights[at]
+            for margin in (*range(MARGIN), *range(MARGIN + GROUPS + 1, SPAN)):
+                value[at, t, margin] = zero
+        return carry
+
+    lax.fori_loop(0, SLOTS * VROWS, clear, 0)
 
     residue = 4 * wrap(a, 4) + b
     along_x = [profile(sub + 8 * g, PX) for g in range(GROUPS)]
@@ -249,30 +238,24 @@
                 for t in range(2):
                     ends = [zero] + turned[t] + [zero]
                     for g in range(GROUPS + 1):
-                        value[from_b, v, t, MARGIN + g] = jnp.where(sub < turn_x, ends[g], ends[g + 1])
+                        value[VROWS * slot + v, t, MARGIN + g] = jnp.where(sub < turn_x, ends[g], ends[g + 1])
             return carry
 
         lax.fori_loop(0, GY, weigh, 0)
 
-    def place_group(half, step, lane_tiles, first):
-        corners = [corner(step, from_b) for from_b in range(GY)]
+    def place_all(half, t):
+        corners = [(4 * step + from_b, corner(step, from_b)) for step in range(4) for from_b in range(GY)]
+        bases = [(VROWS * slot - first_y, first_y, MARGIN - halved(sx, 3)) for slot, (sx, first_y, _, _) in corners]
 
         def place(y, carry):
             places = []
-            for sx, first_y, _, _ in corners:
-                v = y - first_y
-                places.append((jnp.where((v >= 0) & (v < VROWS), v, VROWS), MARGIN - halved(sx, 3)))
-            loaded = [{t: value[s, v, t, pl.ds(at, GX)] for t in lane_tiles} for s, (v, at) in enumerate(places)]
-            sums_of = {}
-            for t in lane_tiles:
-                for block in range(GX):
-                    one, two, three, four = [tiles[t][block] for tiles in loaded]
-                    got = (one + two) + (three + four)
-                    if not first:
-                        got = got + acc[half, y, t, 8 * block : 8 * block + 8, :]
-                    sums_of[t, block] = got
-            for (t, block), got in sums_of.items():
-                acc[half, y, t, 8 * block : 8 * block + 8, :] = got
+            for base, first_y, at in bases:
+                valid = (y >= first_y) & (y < first_y + VROWS)
+                places.append((jnp.where(valid, base + y, SLOTS * VROWS), at))
+            got = [value[v, t, pl.ds(at, GX)] for v, at in places]
+            while len(got) > 1:
+                got = [one + two for one, two in zip(got[::2], got[1::2])]
+            acc[half, y, t] = got[0]
             return carry
 
         lax.fori_loop(0, 8, place, 0)
@@ -295,7 +278,7 @@
             rows = slice(8 * block, 8 * block + 8)
             up, low = zero, zero
             for y in range(8):
-                turned = acc[half, y, 1, rows, :]
+                turned = acc[half, y, 1, block]
                 turned = pltpu.roll(turned, 16 * y, 1) if y else turned
                 up = jnp.where(lane // 16 == y, turned, up)
                 low = jnp.where(lane // 16 == (y + 7) % 8, turned, low)
@@ -326,7 +309,7 @@
             back = (128 - 16 * y) % 128
             ends = (pltpu.roll(up, back, 1), pltpu.roll(low, back, 1)) if y else (up, low)
             more = jnp.where(lane < 16, ends[0], jnp.where(lane >= 112, ends[1], 0.0))
-            cells.append(acc[half, y, 0, rows, :] + more)
+            cells.append(acc[half, y, 0, block] + more)
         for y, what in enumerate(cells):
             total[half, pl.ds(pl.multiple_of(64 * block + 8 * y, 8), 8), :] = what
 
@@ -350,15 +333,10 @@
         mine = pl.ds(pl.multiple_of(16 * (GY * a + b), 16), 16)
         parts[half, mine, :] = total[half, mine, :]
 
-    def blend_group(half, step, first):
-        weigh_group(half, step)
-        place_group(half, step, (0, 1), first)
-
-    def blend_last(half, step):
-        weigh_group(half, step)
-        place_group(half, step, (1,), False)
+    def place_and_send_rims(half):
+        place_all(half, 1)
         send_rims(half)
-        place_group(half, step, (0,), False)
+        place_all(half, 0)
 
     def send_rest(*steps):
         for step, turns in turns_of:
@@ -366,19 +344,43 @@
                 piece_copy(0, step, turn).wait_send()
                 piece_copy(1, step, turn).start()
 
-    blend_group(0, 2, True)
+    weigh_group(0, 2)
     send_rest(2)
-    blend_group(0, 1, False)
+    weigh_group(0, 1)
     send_rest(1)
-    blend_group(0, 3, False)
+    weigh_group(0, 3)
     send_rest(3, 0)
-    blend_last(0, 0)
-    blend_group(1, 2, True)
+    weigh_group(0, 0)
+    place_and_send_rims(0)
+    weigh_group(1, 2)
     send_parts(0)
-    blend_group(1, 1, False)
-    blend_group(1, 3, False)
-    blend_last(1, 0)
+    weigh_group(1, 1)
+    weigh_group(1, 3)
+    weigh_group(1, 0)
+    place_and_send_rims(1)
     send_parts(1)
+
+    for offset in range(3 * PX):
+        table[offset] = profile(jnp.full((8, 128), offset - PX, jnp.int32), PX)
+
+    def add_weight(index, carry):
+        i, j, at_k = a - 2 + lax.div(index, 9), b - 1 + lax.rem(lax.div(index, 3), 3), k - 1 + lax.rem(index, 3)
+        valid = (i >= 0) & (i < GX) & (j >= 0) & (j < GY) & (at_k >= 0) & (at_k < GZ)
+        i, j, at_k = jnp.clip(i, 0, GX - 1), jnp.clip(j, 0, GY - 1), jnp.clip(at_k, 0, GZ - 1)
+        along_z = profile(BZ * k + lane - start_ref[i, 2, j, at_k], PZ)
+        along_z = along_z * jnp.where(valid, 1.0, 0.0)
+        y = BY * b + sub - start_ref[i, 1, j, at_k]
+        planes = [profile(y + 8 * g, PY) * along_z for g in range(4)]
+        base = jnp.clip(BX * a - start_ref[i, 0, j, at_k] + PX, 0, 2 * PX)
+        new = []
+        for x in range(BX):
+            along_x = table[base + x]
+            new += [carry[4 * x + g] + along_x * planes[g] for g in range(4)]
+        return tuple(new)
+
+    weights = lax.fori_loop(0, 45, add_weight, (zero,) * 32)
+    for at in range(32):
+        sums[at] = weights[at]
 
     for step, turns in turns_of:
         for turn in turns:
@@ -437,8 +439,8 @@
             pltpu.VMEM((3 * PX, 8, 128), F32),
             pltpu.VMEM((32, 8, 128), F32),
             pltpu.VMEM((16, VROWS, 2, GROUPS, 8, 128), F32),
-            pltpu.VMEM((4, VROWS + 1, 2, SPAN, 8, 128), F32),
-            pltpu.VMEM((2, 8, 2, 64, 128), F32),
+            pltpu.VMEM((SLOTS * VROWS + 1, 2, SPAN, 8, 128), F32),
+            pltpu.VMEM((2, 8, 2, GX, 8, 128), F32),
             pltpu.VMEM((2, 2, 64, 128), F32),
             pltpu.VMEM((2, 2, 64, 128), F32),
             pltpu.VMEM((2, 16 * OWNERS, 128), F32),

time: 44.5 us -> 44.5 us (level)
  no operation moved by 1% of the time
where the time goes in v9:
time: 44.5 us; the launch traced here: 44.4 us
  Pallas kernels  42.6 us (96%)
  local copies, waits for them, and re-layouts  1.77 us (4%)
    pallas_call x1, Pallas kernels, per_device(): pl.pallas_call(blend_kernel, out_shape=jax.ShapeDtypeStruct((BX, CLASSES,...  42.6 us
    unnamed x1, local copies, waits for them, and re-layouts  1.77 us

profile of v9, /device:TPU:1, one launch (start us, length us, event | category | flops | bytes accessed | tf_op | source)
XLA Modules:
  0.0 44.4 jit_solution(6878049017347809562)
XLA Ops:
  0.0 42.6 %shard_map.37 = f32[8,3,32,128]{3,2,1,0:T(8,128)} custom-call(s32[8,4,8]{2,1,0:T(4,128)} %owner_hbm.1, s32[8,3,4,8]{3,2,1,0:T(4,128)} %bitcast.7, bf16[3,162,8,128]{3,2,1,0:T(8,128)(2,1)} %bitcast.6), custom_call_target="tpu_custom_call" | custom-call | tf_op jit(solution)/shard_map/pallas_call | solution.py:422
  42.6 1.8 %copy.5 = f32[8,32,3,128]{3,1,2,0:T(8,128)} copy(f32[8,32,3,128]{3,1,2,0:T(8,128)} %bitcast.5) | data formatting | bytes 786432

commit v10 on v9

--- a/solution.py
+++ b/solution.py
@@ -455,7 +455,7 @@
             pltpu.SemaphoreType.DMA((2, OWNERS)),
             pltpu.SemaphoreType.DMA((2, OWNERS)),
         ],
-        compiler_params=pltpu.CompilerParams(collective_id=0, has_side_effects=True, vmem_limit_bytes=62000000),
+        compiler_params=pltpu.CompilerParams(collective_id=0, has_side_effects=True, vmem_limit_bytes=56000000),
     )(patch_owner, jnp.transpose(patch_start, (0, 3, 1, 2)), jnp.transpose(tiles, (0, 2, 1, 3)))
     return jnp.transpose(probs, (0, 2, 1, 3))
 

time: 44.5 us -> 44.2 us (level)
  Pallas kernels: 42.6 us -> 41.8 us
  local copies, waits for them, and re-layouts: 1.77 us -> 2.26 us
    pallas_call x1, Pallas kernels: 42.6 us -> 41.8 us  [per_device(): pl.pallas_call(blend_kernel, out_shape=jax.ShapeDtypeStruct((BX, CLASSES,...]
    unnamed x1 -> x5, local copies, waits for them, and re-layouts: 1.77 us -> 2.26 us
where the time goes in v10:
time: 44.2 us; the launch traced here: 44.1 us
  Pallas kernels  41.8 us (95%)
  local copies, waits for them, and re-layouts  2.26 us (5%)
    pallas_call x1, Pallas kernels, per_device(): pl.pallas_call(blend_kernel, out_shape=jax.ShapeDtypeStruct((BX, CLASSES,...  41.8 us
    unnamed x5, local copies, waits for them, and re-layouts  2.26 us

profile of v10, /device:TPU:1, one launch (start us, length us, event | category | flops | bytes accessed | tf_op | source)
XLA Modules:
  0.0 44.1 jit_solution(5994683576521006149)
XLA Ops:
  0.0 0.0 copy-start
  0.0 0.8 %copy-done = s32[8,4,8,3]{2,1,3,0:T(4,128)S(1)} copy-done((s32[8,4,8,3]{2,1,3,0:T(4,128)S(1)}, s32[8,4,8,3]{2,1,3,0:T(4,128)}, u32[]{:S(2)}) %copy-start) | copy-done | bytes 3096
  0.8 0.0 copy-start.1
  0.8 0.7 %copy-done.1 = s32[8,4,8]{2,1,0:T(4,128)S(1)} copy-done((s32[8,4,8]{2,1,0:T(4,128)S(1)}, s32[8,4,8]{2,1,0:T(4,128)}, u32[]{:S(2)}) %copy-start.1) | copy-done | bytes 1048
  1.5 41.8 %shard_map.37 = f32[8,3,32,128]{3,2,1,0:T(8,128)S(1)} custom-call(s32[8,4,8]{2,1,0:T(4,128)S(1)} %copy-done.1, s32[8,3,4,8]{3,2,1,0:T(4,128)S(1)} %bitcast.6, bf16[3,162,8,128]{3,2,1,0:T(8,128)(2,1)} %bitcast.7), custom_call_target="tpu_custom_call" | custom-call | tf_op jit(solution)/shard_map/pallas_call | solution.py:422
  43.3 0.7 %copy.5 = f32[8,32,3,128]{3,1,2,0:T(8,128)} copy(f32[8,32,3,128]{3,1,2,0:T(8,128)S(1)} %bitcast.5) | data formatting | bytes 786432
Async XLA Ops:
  0.0 0.8 %copy-start = (s32[8,4,8,3]{2,1,3,0:T(4,128)S(1)}, s32[8,4,8,3]{2,1,3,0:T(4,128)}, u32[]{:S(2)}) copy-start(s32[8,4,8,3]{2,1,3,0:T(4,128)} %param.4) | copy-start | bytes 9220
  0.8 0.7 %copy-start.1 = (s32[8,4,8]{2,1,0:T(4,128)S(1)}, s32[8,4,8]{2,1,0:T(4,128)}, u32[]{:S(2)}) copy-start(s32[8,4,8]{2,1,0:T(4,128)} %owner_hbm.1) | copy-start | bytes 3076

commit v11 on v10

--- a/solution.py
+++ b/solution.py
@@ -456,7 +456,11 @@
             pltpu.SemaphoreType.DMA((2, OWNERS)),
         ],
         compiler_params=pltpu.CompilerParams(collective_id=0, has_side_effects=True, vmem_limit_bytes=56000000),
-    )(patch_owner, jnp.transpose(patch_start, (0, 3, 1, 2)), jnp.transpose(tiles, (0, 2, 1, 3)))
+    )(
+        pltpu.with_memory_space_constraint(patch_owner, pltpu.HBM),
+        pltpu.with_memory_space_constraint(jnp.transpose(patch_start, (0, 3, 1, 2)), pltpu.HBM),
+        jnp.transpose(tiles, (0, 2, 1, 3)),
+    )
     return jnp.transpose(probs, (0, 2, 1, 3))
 
 

time: 44.2 us -> 42.7 us (0.966)
  local copies, waits for them, and re-layouts: 2.26 us -> 0.75 us
    unnamed x5 -> x1, local copies, waits for them, and re-layouts: 2.26 us -> 0.75 us
where the time goes in v11:
time: 42.7 us; the launch traced here: 42.6 us
  Pallas kernels  41.8 us (98%)
  local copies, waits for them, and re-layouts  0.75 us (2%)
    pallas_call x1, Pallas kernels, per_device(): pl.pallas_call(blend_kernel, out_shape=jax.ShapeDtypeStruct((BX, CLASSES,...  41.8 us

profile of v11, /device:TPU:1, one launch (start us, length us, event | category | flops | bytes accessed | tf_op | source)
XLA Modules:
  0.0 42.6 jit_solution(1906287676175357661)
XLA Ops:
  0.0 41.8 %shard_map.37 = f32[8,3,32,128]{3,2,1,0:T(8,128)S(1)} custom-call(s32[8,4,8]{2,1,0:T(4,128)} %owner_hbm.1, s32[8,3,4,8]{3,2,1,0:T(4,128)} %bitcast.7, bf16[3,162,8,128]{3,2,1,0:T(8,128)(2,1)} %bitcast.6), custom_call_target="tpu_custom_call" | custom-call | tf_op jit(solution)/shard_map/pallas_call | solution.py:422
  41.8 0.7 %copy.5 = f32[8,32,3,128]{3,1,2,0:T(8,128)} copy(f32[8,32,3,128]{3,1,2,0:T(8,128)S(1)} %bitcast.5) | data formatting | bytes 786432

commit v12 on v11

--- a/solution.py
+++ b/solution.py
@@ -144,7 +144,15 @@
             cut(half, 4 * wrap(a + step, 4) + wrap(b + turn, GY), store)
             return carry
 
-        lax.fori_loop(0 if step else 1, GY, cut_one, 0)
+        if half == 0 and step == 2:
+            for at, turn in enumerate(ORDER):
+                cut_one(turn, 0)
+                if at == 1:
+                    pl.semaphore_wait(barrier, len(near))
+                if at:
+                    piece_copy(0, step, ORDER[at - 1]).start()
+        else:
+            lax.fori_loop(0 if step else 1, GY, cut_one, 0)
 
     def cut_own(half):
         def store(tile, what):
@@ -154,9 +162,7 @@
 
     for step, turns in turns_of:
         cut_step(0, step)
-        if step == 2:
-            pl.semaphore_wait(barrier, len(near))
-        for turn in turns:
+        for turn in turns[3:] if step == 2 else turns:
             piece_copy(0, step, turn).start()
     cut_own(0)
     for step, _ in turns_of:
@@ -385,9 +391,9 @@
     for step, turns in turns_of:
         for turn in turns:
             piece_copy(1, step, turn).wait_send()
-    for half in range(2):
-
-        def await_parts(far, carry, half=half):
+
+    def await_parts(half):
+        def await_block(far, carry):
             for turn in range(GY - 1):
                 part_copy(half, far, turn).wait()
 
@@ -397,24 +403,29 @@
 
             return carry
 
-        lax.fori_loop(0, GX, await_parts, 0)
-
+        lax.fori_loop(0, GX, await_block, 0)
+
+    def score(half, x, quarter):
+        row = 8 * 16 * (quarter % 2) + 8 * (quarter // 2) + x
+        one, two = [parts[half, pl.ds(row + more, 8, stride=16), :] for more in (0, 256)]
+        return (one + two) / sums[4 * x + quarter]
+
+    await_parts(0)
     for x in range(BX):
-        for h in range(2):
-            for g in range(2):
-                row = 8 * g * 16 + 8 * h + x
-                norm = sums[4 * x + 2 * h + g]
-                d1, d2 = [
-                    (parts[half, pl.ds(row, 8, stride=16), :] + parts[half, pl.ds(row + 256, 8, stride=16), :]) / norm
-                    for half in range(2)
-                ]
-                top = jnp.maximum(jnp.maximum(d1, d2), 0.0)
-                e0, e1, e2 = jnp.exp(-top), jnp.exp(d1 - top), jnp.exp(d2 - top)
-                scale = 1.0 / (e0 + e1 + e2)
-                rows = slice(16 * h + 8 * g, 16 * h + 8 * g + 8)
-                out_ref[x, 0, rows, :] = e0 * scale
-                out_ref[x, 1, rows, :] = e1 * scale
-                out_ref[x, 2, rows, :] = e2 * scale
+        scores = [score(0, x, quarter) for quarter in range(4)]
+        for quarter in range(4):
+            acc[0, x, 0, quarter] = scores[quarter]
+    await_parts(1)
+    for x in range(BX):
+        for quarter in range(4):
+            d1, d2 = acc[0, x, 0, quarter], score(1, x, quarter)
+            top = jnp.maximum(jnp.maximum(d1, d2), 0.0)
+            e0, e1, e2 = jnp.exp(-top), jnp.exp(d1 - top), jnp.exp(d2 - top)
+            scale = 1.0 / (e0 + e1 + e2)
+            rows = slice(8 * quarter, 8 * quarter + 8)
+            out_ref[x, 0, rows, :] = e0 * scale
+            out_ref[x, 1, rows, :] = e1 * scale
+            out_ref[x, 2, rows, :] = e2 * scale
 
 
 def per_device(patch_logits, patch_start, patch_owner):

time: 42.7 us -> 42.7 us (level)
  no operation moved by 1% of the time
where the time goes in v12:
time: 42.7 us; the launch traced here: 42.6 us
  Pallas kernels  41.8 us (98%)
  local copies, waits for them, and re-layouts  0.75 us (2%)
    pallas_call x1, Pallas kernels, per_device(): pl.pallas_call(blend_kernel, out_shape=jax.ShapeDtypeStruct((BX, CLASSES,...  41.8 us

profile of v12, /device:TPU:1, one launch (start us, length us, event | category | flops | bytes accessed | tf_op | source)
XLA Modules:
  0.0 42.6 jit_solution(8491206843576379523)
XLA Ops:
  0.0 41.8 %shard_map.37 = f32[8,3,32,128]{3,2,1,0:T(8,128)S(1)} custom-call(s32[8,4,8]{2,1,0:T(4,128)} %owner_hbm.1, s32[8,3,4,8]{3,2,1,0:T(4,128)} %bitcast.7, bf16[3,162,8,128]{3,2,1,0:T(8,128)(2,1)} %bitcast.6), custom_call_target="tpu_custom_call" | custom-call | tf_op jit(solution)/shard_map/pallas_call | solution.py:433
  41.8 0.7 %copy.5 = f32[8,32,3,128]{3,1,2,0:T(8,128)} copy(f32[8,32,3,128]{3,1,2,0:T(8,128)S(1)} %bitcast.5) | data formatting | bytes 786432

commit v13 on v12

--- a/solution.py
+++ b/solution.py
@@ -60,9 +60,6 @@
     near = [
         (wrap(a + dz, GX), wrap(b + db, GY), k) for dz in (0, 1, -1, 2, -2) for db in range(GY) if dz or db
     ] + [(a, b, above), (a, b, below)]
-    barrier = pltpu.get_barrier_semaphore()
-    for to in near:
-        pl.semaphore_signal(barrier, inc=1, device_id=to, device_id_type=MESH)
     load = pltpu.make_async_copy(x_ref, patch, in_sem)
     load.start()
     indices = [
@@ -71,6 +68,9 @@
     ]
     for copy in indices:
         copy.start()
+    barrier = pltpu.get_barrier_semaphore()
+    for to in near:
+        pl.semaphore_signal(barrier, inc=1, device_id=to, device_id_type=MESH)
 
     lane, sub = iota(1), iota(0)
     zero = jnp.zeros((8, 128), F32)

time: 42.7 us -> 42.8 us (level)
  no operation moved by 1% of the time
where the time goes in v13:
time: 42.8 us; the launch traced here: 42.6 us
  Pallas kernels  41.9 us (98%)
  local copies, waits for them, and re-layouts  0.75 us (2%)
    pallas_call x1, Pallas kernels, per_device(): pl.pallas_call(blend_kernel, out_shape=jax.ShapeDtypeStruct((BX, CLASSES,...  41.9 us

profile of v13, /device:TPU:1, one launch (start us, length us, event | category | flops | bytes accessed | tf_op | source)
XLA Modules:
  0.0 42.6 jit_solution(12332311027314405971)
XLA Ops:
  0.0 41.9 %shard_map.37 = f32[8,3,32,128]{3,2,1,0:T(8,128)S(1)} custom-call(s32[8,4,8]{2,1,0:T(4,128)} %owner_hbm.1, s32[8,3,4,8]{3,2,1,0:T(4,128)} %bitcast.7, bf16[3,162,8,128]{3,2,1,0:T(8,128)(2,1)} %bitcast.6), custom_call_target="tpu_custom_call" | custom-call | tf_op jit(solution)/shard_map/pallas_call | solution.py:433
  41.9 0.7 %copy.5 = f32[8,32,3,128]{3,1,2,0:T(8,128)} copy(f32[8,32,3,128]{3,1,2,0:T(8,128)S(1)} %bitcast.5) | data formatting | bytes 786432
